TPU v7x, 256 devices: a whole 4x4x8 slice. The times are simulated.
256 devices in a mesh: pts: 32 (over z, y_lo, core), grp: 8 (over y_hi, x).
Axes of the slice: x: 4, y: 4 (y_hi: 2, y_lo: 2; y = y_hi * 2 + y_lo), z: 8, core: 2. Of those that a mesh axis runs over, the one named last changes fastest.
Arguments:
- occ_orbitals: bfloat16 [8192, 1024], P('pts'), may hold values from -0.1875 to 0.1875
- virt_orbitals: bfloat16 [8192, 1024], P('pts'), may hold values from -0.1875 to 0.1875
- columns: bfloat16 [8192, 512], P('pts'), may hold values from -6 to 6
- occ_energies: float32 [1024], replicated, may hold values from -3 to -0.1
- vir_energies: float32 [1024], replicated, may hold values from 0.1 to 3
- tau_index: int32 [8], replicated, may hold values from 0 to 15, as said below
- quad_weights: float32 [8], replicated, may hold values from 0.05 to 0.5
- frequencies: float32 [2], replicated, may hold values from 0.2 to 2
- distance_kept: int32 [32], replicated, may hold values 0 or 1
Outputs:
- response: float32 [2, 512, 8192], P(None, 'grp', 'pts')
Inputs may be any that keep to these rules, and one draw needn't show every extreme that they name: `tau_index`: all entries differ; 0 and 15 are always among them.
All inputs are finite; a program needn't handle non-finite values.
Results may differ from a plain program's by a relative error of at most 0.0026.
Values may be sent and summed in bfloat16 or wider, within the bound.
No kernel may reach another device: no remote copies, remote signals or barrier semaphores. Data moves between devices by JAX's collectives and lax.ppermute only.
A program may use at most 64 MiB of HBM per device.

v0:
```python
import math

import jax
import jax.numpy as jnp
from jax import lax
from jax.experimental import pallas as pl
from jax.experimental.pallas import tpu as pltpu
from jax.sharding import Mesh, PartitionSpec as P


AXES = ("z", "yl", "c", "yh", "x")
SIZES = (8, 2, 2, 2, 4)
NZ, NYL, NC, NYH, NX = SIZES
PLANES = (
    (0, 5, 6, 3, 4, 1, 2, 7),
    (1, 3, 7, 5, 2, 0, 4, 6),
    (2, 6, 4, 1, 7, 3, 5, 0),
    (3, 7, 1, 4, 6, 2, 0, 5),
    (4, 1, 2, 7, 0, 5, 6, 3),
    (5, 0, 3, 6, 1, 4, 7, 2),
    (6, 4, 0, 2, 5, 7, 3, 1),
    (7, 2, 5, 0, 3, 6, 1, 4),
)
TILE = 128
VMEM = pl.BlockSpec(memory_space=pltpu.VMEM)
SMEM = pl.BlockSpec(memory_space=pltpu.SMEM)
MIB = 1024 * 1024


def place(at):
    index = 0
    for value, size in zip(at, SIZES):
        index = index * size + value % size
    return index


def everywhere(at=()):
    if len(at) == len(SIZES):
        return [at]
    return [full for i in range(SIZES[len(at)]) for full in everywhere((*at, i))]


def take(array, source):
    return lax.ppermute(array, AXES, [(place(source(*at)), place(at)) for at in everywhere()])


def from_plane(array):
    return take(array, lambda z, yl, c, yh, x: (PLANES[yh * NX + x][z], yl, c, yh, x))


def from_core(array):
    return take(array, lambda z, yl, c, yh, x: (z, yl, c + 1, yh, x))


def from_y(array, by):
    def source(z, yl, c, yh, x):
        y = (yh * NYL + yl + by) % (NYH * NYL)
        return z, y % NYL, c, y // NYL, x

    return take(array, source)


def cost(flops):
    return pl.CostEstimate(flops=int(flops), bytes_accessed=4 * MIB, transcendentals=0)


def scale_rows(source, decay, out):
    step = 16

    def body(i):
        rows = pl.ds(pl.multiple_of(i * step, step), step)
        values = source[rows, :].astype(jnp.float32)
        for k in range(out.shape[0]):
            out[k, rows, :] = (values * decay[k : k + 1, :]).astype(jnp.bfloat16)

    pl.loop(0, source.shape[0] // step)(body)


def scale_kernel(occ_ref, vir_ref, occ_decay_ref, vir_decay_ref, occ_out, vir_out):
    scale_rows(occ_ref, occ_decay_ref, occ_out)
    scale_rows(vir_ref, vir_decay_ref, vir_out)


def scaled(occ, vir, occ_decay, vir_decay):
    shape = jax.ShapeDtypeStruct((occ_decay.shape[0], *occ.shape), jnp.bfloat16)
    return pl.pallas_call(
        scale_kernel,
        out_shape=(shape, shape),
        in_specs=[VMEM] * 4,
        out_specs=(VMEM, VMEM),
        compiler_params=pltpu.CompilerParams(vmem_limit_bytes=12 * MIB),
        cost_estimate=cost(1e8),
    )(occ, vir, occ_decay, vir_decay)


def mark_kernel(cos_ref, kept_ref, planes_ref, cos_out, kept_out):
    z, yl, c, yh, x = (lax.axis_index(name) for name in AXES)
    count = kept_ref.shape[0]
    half = kept_out.shape[1] // 2
    plane = planes_ref[(yh * NX + x) * NZ + z]
    for i, row_yl in enumerate((yl, 1 - yl)):
        row = (z * NYL + row_yl) * NC + c
        for j, from_c in enumerate((c, 1 - c)):
            block = (plane * NYL + yl) * NC + from_c
            kept = kept_ref[(block - row + count) % count].astype(jnp.float32)
            kept_out[i : i + 1, j * half : (j + 1) * half] = jnp.full((1, half), kept, jnp.float32)
    for i in range(cos_out.shape[0]):
        cos_out[i : i + 1, :] = jnp.full((1, cos_out.shape[1]), cos_ref[i], jnp.float32)


def marked(cosine, kept, planes, points):
    return pl.pallas_call(
        mark_kernel,
        out_shape=(
            jax.ShapeDtypeStruct((cosine.shape[0], points), jnp.float32),
            jax.ShapeDtypeStruct((8, 2 * points), jnp.float32),
        ),
        in_specs=[SMEM] * 3,
        out_specs=(VMEM, VMEM),
        compiler_params=pltpu.CompilerParams(vmem_limit_bytes=2 * MIB),
        cost_estimate=cost(1e6),
    )(cosine, kept, planes)


CONTRACT = (((1,), (1,)), ((), ()))


def green(scaled_ref, tile, s_ref):
    taus, _, states = scaled_ref.shape
    rows = pl.ds(pl.multiple_of(tile * TILE, TILE), TILE)
    left = scaled_ref[:, rows, :].reshape(taus * TILE, states)
    return lax.dot_general(left, s_ref[...], CONTRACT, preferred_element_type=jnp.float32)


def occ_kernel(own_ref, near_ref, s_own, s_other, out_ref):
    tiles = own_ref.shape[1] // TILE
    points = s_own.shape[0]
    for i, source in enumerate((own_ref, near_ref)):

        def body(t, i=i, source=source):
            for j, s_ref in enumerate((s_own, s_other)):
                out_ref[i * tiles + t, :, j * points : (j + 1) * points] = green(source, t, s_ref)

        pl.loop(0, tiles)(body)


def occ_term(own, near, s_own, s_other):
    taus, points, states = own.shape
    return pl.pallas_call(
        occ_kernel,
        out_shape=jax.ShapeDtypeStruct((2 * points // TILE, taus * TILE, 2 * points), jnp.float32),
        in_specs=[VMEM] * 4,
        out_specs=VMEM,
        compiler_params=pltpu.CompilerParams(vmem_limit_bytes=26 * MIB),
        cost_estimate=cost(8 * taus * points * points * states),
    )(own, near, s_own, s_other)


def chi_kernel(first, row, cos_ref, kept_ref, scaled_ref, s_own, s_other, occ_ref, out_ref):
    taus, points, _ = scaled_ref.shape

    def body(t):
        rows = pl.ds(pl.multiple_of(t * TILE, TILE), TILE)
        for j, s_ref in enumerate((s_own, s_other)):
            here = slice(j * points, (j + 1) * points)
            product = green(scaled_ref, t, s_ref) * occ_ref[first + t, :, here]
            product = product.reshape(taus, TILE, points)
            for w in range(2):
                chi = cos_ref[w * taus : w * taus + 1, :] * product[0]
                for k in range(1, taus):
                    chi = chi + cos_ref[w * taus + k : w * taus + k + 1, :] * product[k]
                chi = chi * kept_ref[row : row + 1, here]
                high = chi.astype(jnp.bfloat16)
                out_ref[w, 0, rows, here] = high
                out_ref[w, 1, rows, here] = (chi - high.astype(jnp.float32)).astype(jnp.bfloat16)

    pl.loop(0, points // TILE)(body)


def chi_term(row, cos_rows, marks, vir_scaled, s_own, s_other, green_occ):
    taus, points, states = vir_scaled.shape

    def kernel(*refs):
        chi_kernel(row * (points // TILE), row, *refs)

    return pl.pallas_call(
        kernel,
        out_shape=jax.ShapeDtypeStruct((2, 2, points, 2 * points), jnp.bfloat16),
        in_specs=[VMEM] * 6,
        out_specs=VMEM,
        compiler_params=pltpu.CompilerParams(vmem_limit_bytes=24 * MIB),
        cost_estimate=cost(4 * taus * points * points * states),
    )(cos_rows, marks, vir_scaled, s_own, s_other, green_occ)


def answer_kernel(own_ref, near_ref, s_own, s_other, out_ref):
    yl = lax.axis_index("yl")
    points = s_own.shape[0]
    _, groups, _, width, _ = out_ref.shape
    for slot, chi_ref in ((yl, own_ref), (1 - yl, near_ref)):
        for w in range(2):
            both = chi_ref[w].reshape(2 * points, 2 * points)
            answer = jnp.dot(both[:, :points], s_own[...], preferred_element_type=jnp.float32)
            answer = answer + jnp.dot(both[:, points:], s_other[...], preferred_element_type=jnp.float32)
            answer = answer[:points] + answer[points:]
            out_ref[slot, :, w] = answer.T.astype(jnp.bfloat16).reshape(groups, width, points)


def answer_term(own, near, s_own, s_other):
    points, columns = s_own.shape
    groups = NYH * NX
    return pl.pallas_call(
        answer_kernel,
        out_shape=jax.ShapeDtypeStruct((NYL, groups, 2, columns // groups, points), jnp.bfloat16),
        in_specs=[VMEM] * 4,
        out_specs=VMEM,
        compiler_params=pltpu.CompilerParams(vmem_limit_bytes=16 * MIB),
        cost_estimate=cost(32 * points * points * columns),
    )(own, near, s_own, s_other)


def per_device(
    occ_orbitals,
    virt_orbitals,
    columns,
    occ_energies,
    vir_energies,
    tau_index,
    quad_weights,
    frequencies,
    distance_kept,
):
    points = occ_orbitals.shape[0]
    occ_s = from_plane(occ_orbitals)
    occ_near = from_y(occ_orbitals, 1)
    vir_near = from_y(virt_orbitals, -1)
    vir_s = from_plane(virt_orbitals)
    col_s = from_plane(columns)
    occ_t = from_core(occ_s)
    vir_t = from_core(vir_s)
    col_t = from_core(col_s)

    times = 0.05 * jnp.exp(tau_index.astype(jnp.float32) * jnp.float32(math.log(1.5)))
    cosine = (-quad_weights[None, :] * jnp.cos(frequencies[:, None] * times[None, :])).reshape(-1)
    occ_decay = jnp.exp(occ_energies[None, :] * times[:, None])
    vir_decay = jnp.exp(-vir_energies[None, :] * times[:, None])
    planes = jnp.array(PLANES, jnp.int32).reshape(-1)
    cos_rows, marks = marked(cosine, distance_kept, planes, points)
    occ_own, vir_own = scaled(occ_orbitals, virt_orbitals, occ_decay, vir_decay)
    occ_next, vir_next = scaled(occ_near, vir_near, occ_decay, vir_decay)
    green_occ = occ_term(occ_own, occ_next, occ_s, occ_t)
    chi_own = chi_term(0, cos_rows, marks, vir_own, vir_s, vir_t, green_occ)
    chi_near = chi_term(1, cos_rows, marks, vir_next, vir_s, vir_t, green_occ)
    parts = answer_term(chi_own, chi_near, col_s, col_t)
    parts = parts.reshape(-1, *parts.shape[2:])
    spread = lax.all_to_all(parts, ("yl", "yh", "x"), split_axis=0, concat_axis=0, tiled=True)
    return spread.astype(jnp.float32).sum(axis=0)


def solution(mesh):
    fine = Mesh(mesh.devices.reshape(SIZES), AXES)

    rows = P(("z", "yl", "c"), None)
    return jax.shard_map(
        per_device,
        mesh=fine,
        in_specs=(rows, rows, rows, P(), P(), P(), P(), P(), P()),
        out_specs=P(None, ("yh", "x"), ("z", "yl", "c")),
        check_vma=False,
    )
```

profile of v0, /device:TPU:1, one launch (start us, length us, event | category | flops | bytes accessed | tf_op | source)
XLA Modules:
  0.0 78.1 jit_solution(8315557285422161681)
XLA Ops:
  0.0 1.7 %collective-permute-start.4 = (bf16[256,1024]{1,0:T(8,128)(2,1)}, bf16[256,1024]{1,0:T(8,128)(2,1)S(1)}, u32[]{:S(2)}, u32[]{:S(2)}) collective-permute-start(bf16[256,1024]{1,0:T(8,128)(2,1)} %occ_ref.1), channel_id=1, source_target_pairs={{0,0},{33,1},{66,2},{99,3},{132,4},{165,5},{198,6},{231,7},{8,8},{... | collective-permute-start | bytes 1572872 | tf_op jit(solution)/shard_map/ppermute | solution.py:44
  1.7 1.7 %collective-permute-start = (bf16[256,1024]{1,0:T(8,128)(2,1)}, bf16[256,1024]{1,0:T(8,128)(2,1)S(1)}, u32[]{:S(2)}, u32[]{:S(2)}) collective-permute-start(bf16[256,1024]{1,0:T(8,128)(2,1)} %vir_ref.1), channel_id=1, source_target_pairs={{0,0},{33,1},{66,2},{99,3},{132,4},{165,5},{198,6},{231,7},{8,8},{... | collective-permute-start | bytes 1572872 | tf_op jit(solution)/shard_map/ppermute | solution.py:44
  3.4 11.0 %collective-permute-start.2 = (bf16[256,1024]{1,0:T(8,128)(2,1)}, bf16[256,1024]{1,0:T(8,128)(2,1)S(1)}, u32[]{:S(2)}, u32[]{:S(2)}) collective-permute-start(bf16[256,1024]{1,0:T(8,128)(2,1)} %occ_ref.1), channel_id=1, source_target_pairs={{16,0},{17,1},{18,2},{19,3},{20,4},{21,5},{22,6},{23,7},{24,8},{25... | collective-permute-start | bytes 1572872 | tf_op jit(solution)/shard_map/ppermute | solution.py:44
  14.4 0.0 collective-permute-start.3
  14.4 1.6 %collective-permute-start.6 = (bf16[256,512]{1,0:T(8,128)(2,1)}, bf16[256,512]{1,0:T(8,128)(2,1)S(1)}, u32[]{:S(2)}, u32[]{:S(2)}) collective-permute-start(bf16[256,512]{1,0:T(8,128)(2,1)} %param.12), channel_id=1, source_target_pairs={{0,0},{33,1},{66,2},{99,3},{132,4},{165,5},{198,6},{231,7},{8,8},{... | collective-permute-start | bytes 786440 | tf_op jit(solution)/shard_map/ppermute | solution.py:44
  16.0 0.0 collective-permute-done.4.s_own
  16.0 1.2 %collective-permute-start.5 = (bf16[256,1024]{1,0:T(8,128)(2,1)S(1)}, bf16[256,1024]{1,0:T(8,128)(2,1)S(1)}, u32[]{:S(2)}, u32[]{:S(2)}) collective-permute-start(bf16[256,1024]{1,0:T(8,128)(2,1)S(1)} %collective-permute-done.4.s_own), channel_id=1, source_target_pairs={{8,0},{9,1},{10,2},{11,3},{12,4},{13,5},{14,6},{15,7},{0,8},{1,9},... | collective-permute-start | bytes 1572872 | tf_op jit(solution)/shard_map/ppermute | solution.py:44
  17.2 0.7 exponential_multiply_fusion
  17.9 0.7 neg.9
  18.6 0.8 multiply_exponential_fusion
  19.3 0.7 neg.8
  20.0 0.0 collective-permute-done.refs_3_
  20.0 0.0 collective-permute-start.1
  20.0 0.8 cosine_multiply_fusion
  20.8 0.1 mul.64.cos_ref
  20.9 0.0 copy-start.2
  20.9 0.7 copy-done.2
  21.5 0.0 copy-start.3
  21.5 0.7 copy-done.3
  22.2 0.6 shard_map.100
  22.8 0.0 copy-start
  22.8 1.0 %copy-done = bf16[256,1024]{1,0:T(8,128)(2,1)S(1)} copy-done((bf16[256,1024]{1,0:T(8,128)(2,1)S(1)}, bf16[256,1024]{1,0:T(8,128)(2,1)}, u32[]{:S(2)}) %copy-start) | copy-done | bytes 524312
  23.8 0.0 copy-start.1
  23.8 1.0 %copy-done.1 = bf16[256,1024]{1,0:T(8,128)(2,1)S(1)} copy-done((bf16[256,1024]{1,0:T(8,128)(2,1)S(1)}, bf16[256,1024]{1,0:T(8,128)(2,1)}, u32[]{:S(2)}) %copy-start.1) | copy-done | bytes 524312
  24.9 1.4 %shard_map.101 = (bf16[8,256,1024]{2,1,0:T(8,128)(2,1)S(1)}, bf16[8,256,1024]{2,1,0:T(8,128)(2,1)S(1)}) custom-call(bf16[256,1024]{1,0:T(8,128)(2,1)S(1)} %copy-done, bf16[256,1024]{1,0:T(8,128)(2,1)S(1)} %copy-done.1, f32[8,1024]{1,0:T(8,128)S(1)} %get-tuple-element.18.occ_decay_ref, f32[8,1024]{1,0:T(8,128)S(1)} %get-tuple-element.17.vir_decay_ref), custom_call_target="tpu_custom_call" | custom-call | flops 100000000 | bytes 4194304 | tf_op jit(solution)/shard_map/pallas_call | solution.py:86
  26.2 0.0 collective-permute-done.6.s_own
  26.2 0.6 collective-permute-start.7
  26.8 0.0 collective-permute-done.2.occ_ref
  26.8 1.2 %collective-permute-done.3.vir_ref = bf16[256,1024]{1,0:T(8,128)(2,1)S(1)} collective-permute-done((bf16[256,1024]{1,0:T(8,128)(2,1)}, bf16[256,1024]{1,0:T(8,128)(2,1)S(1)}, u32[]{:S(2)}, u32[]{:S(2)}) %collective-permute-start.3) | collective-permute-done | bytes 524320 | tf_op jit(solution)/shard_map/ppermute | solution.py:44
  28.0 1.4 %shard_map.102 = (bf16[8,256,1024]{2,1,0:T(8,128)(2,1)S(1)}, bf16[8,256,1024]{2,1,0:T(8,128)(2,1)S(1)}) custom-call(bf16[256,1024]{1,0:T(8,128)(2,1)S(1)} %collective-permute-done.2.occ_ref, bf16[256,1024]{1,0:T(8,128)(2,1)S(1)} %collective-permute-done.3.vir_ref, f32[8,1024]{1,0:T(8,128)S(1)} %get-tuple-element.18.occ_decay_ref, ...), custom_call_target="tpu_custom_call" | custom-call | flops 100000000 | bytes 4194304 | tf_op jit(solution)/shard_map/pallas_call | solution.py:86
  29.4 0.0 collective-permute-done.5.s_other
  29.4 5.1 %shard_map.103.refs_5_ = f32[4,1024,512]{2,1,0:T(8,128)S(1)} custom-call(bf16[8,256,1024]{2,1,0:T(8,128)(2,1)S(1)} %get-tuple-element.14.own_ref, bf16[8,256,1024]{2,1,0:T(8,128)(2,1)S(1)} %get-tuple-element.15.near_ref, bf16[256,1024]{1,0:T(8,128)(2,1)S(1)} %collective-permute-done.4.s_own, bf16[256,1024]{1,0:T(8,128)(2,1)S(1)} %collective-permute-done.5.s_other), custom_call_target="tpu_custom_call" | custom-call | flops 4294967296 | bytes 4194304 | tf_op jit(solution)/shard_map/pallas_call | solution.py:149
  34.6 0.0 collective-permute-done.1.refs_4_
  34.6 3.0 %shard_map.105.near_ref = bf16[2,2,256,512]{3,2,1,0:T(8,128)(2,1)S(1)} custom-call(f32[16,256]{1,0:T(8,128)S(1)} %get-tuple-element.11.refs_0_, f32[8,512]{1,0:T(8,128)S(1)} %get-tuple-element.12.refs_1_, bf16[8,256,1024]{2,1,0:T(8,128)(2,1)S(1)} %get-tuple-element.16.refs_2_, bf16[256,1024]{1,0:T(8,128)(2,1)S(1)} %collective-permute-done.refs_3_, ...), custom_call_target="tpu_custom_call" | custom-call | flops 2147483648 | bytes 4194304 | tf_op jit(solution)/shard_map/pallas_call | solution.py:186
  37.6 3.0 %shard_map.104.own_ref = bf16[2,2,256,512]{3,2,1,0:T(8,128)(2,1)S(1)} custom-call(f32[16,256]{1,0:T(8,128)S(1)} %get-tuple-element.11.refs_0_, f32[8,512]{1,0:T(8,128)S(1)} %get-tuple-element.12.refs_1_, bf16[8,256,1024]{2,1,0:T(8,128)(2,1)S(1)} %get-tuple-element.13.refs_2_, bf16[256,1024]{1,0:T(8,128)(2,1)S(1)} %collective-permute-done.refs_3_, ...), custom_call_target="tpu_custom_call" | custom-call | flops 2147483648 | bytes 4194304 | tf_op jit(solution)/shard_map/pallas_call | solution.py:186
  40.6 0.0 collective-permute-done.7.s_other
  40.7 1.3 %shard_map.106 = bf16[2,8,2,64,256]{4,3,2,1,0:T(8,128)(2,1)S(1)} custom-call(bf16[2,2,256,512]{3,2,1,0:T(8,128)(2,1)S(1)} %shard_map.104.own_ref, bf16[2,2,256,512]{3,2,1,0:T(8,128)(2,1)S(1)} %shard_map.105.near_ref, bf16[256,512]{1,0:T(8,128)(2,1)S(1)} %collective-permute-done.6.s_own, bf16[256,512]{1,0:T(8,128)(2,1)S(1)} %collective-permute-done.7.s_other), custom_call_target="tpu_custom_call" | custom-call | flops 1073741824 | bytes 4194304 | tf_op jit(solution)/shard_map/pallas_call | solution.py:212
  42.0 35.3 %all_to_all.5 = bf16[16,2,64,256]{3,2,1,0:T(8,128)(2,1)S(1)} all-to-all(bf16[16,2,64,256]{3,2,1,0:T(8,128)(2,1)S(1)} %bitcast.1), channel_id=1, replica_groups=mesh['z'=8,'yl'=2,'c'=2,'yh'=2,'x'=4] {'yl','yh','x'}, dimensions={0} | all-to-all | bytes 2097152 | tf_op jit(solution)/shard_map/all_to_all | solution.py:256
  77.3 0.8 %convert_reduce_fusion = f32[2,64,256]{2,1,0:T(8,128)} fusion(bf16[16,2,64,256]{3,2,1,0:T(8,128)(2,1)S(1)} %all_to_all.5), kind=kLoop, calls=%fused_computation | loop fusion | flops 1015808 | bytes 1179648 | tf_op jit(solution)/shard_map/reduce_sum | solution.py:257
Async XLA Ops:
  0.0 16.0 %collective-permute-start.4 = (bf16[256,1024]{1,0:T(8,128)(2,1)}, bf16[256,1024]{1,0:T(8,128)(2,1)S(1)}, u32[]{:S(2)}, u32[]{:S(2)}) collective-permute-start(bf16[256,1024]{1,0:T(8,128)(2,1)} %occ_ref.1), channel_id=1, source_target_pairs={{0,0},{33,1},{66,2},{99,3},{132,4},{165,5},{198,6},{231,7},{8,8},{... | collective-permute-start | bytes 1572872 | tf_op jit(solution)/shard_map/ppermute | solution.py:44
  1.7 18.3 %collective-permute-start = (bf16[256,1024]{1,0:T(8,128)(2,1)}, bf16[256,1024]{1,0:T(8,128)(2,1)S(1)}, u32[]{:S(2)}, u32[]{:S(2)}) collective-permute-start(bf16[256,1024]{1,0:T(8,128)(2,1)} %vir_ref.1), channel_id=1, source_target_pairs={{0,0},{33,1},{66,2},{99,3},{132,4},{165,5},{198,6},{231,7},{8,8},{... | collective-permute-start | bytes 1572872 | tf_op jit(solution)/shard_map/ppermute | solution.py:44
  3.4 23.4 %collective-permute-start.2 = (bf16[256,1024]{1,0:T(8,128)(2,1)}, bf16[256,1024]{1,0:T(8,128)(2,1)S(1)}, u32[]{:S(2)}, u32[]{:S(2)}) collective-permute-start(bf16[256,1024]{1,0:T(8,128)(2,1)} %occ_ref.1), channel_id=1, source_target_pairs={{16,0},{17,1},{18,2},{19,3},{20,4},{21,5},{22,6},{23,7},{24,8},{25... | collective-permute-start | bytes 1572872 | tf_op jit(solution)/shard_map/ppermute | solution.py:44
  14.4 13.7 %collective-permute-start.3 = (bf16[256,1024]{1,0:T(8,128)(2,1)}, bf16[256,1024]{1,0:T(8,128)(2,1)S(1)}, u32[]{:S(2)}, u32[]{:S(2)}) collective-permute-start(bf16[256,1024]{1,0:T(8,128)(2,1)} %vir_ref.1), channel_id=1, source_target_pairs={{20,0},{21,1},{22,2},{23,3},{16,4},{17,5},{18,6},{19,7},{28,8},{29... | collective-permute-start | bytes 1572872 | tf_op jit(solution)/shard_map/ppermute | solution.py:44
  14.4 11.8 %collective-permute-start.6 = (bf16[256,512]{1,0:T(8,128)(2,1)}, bf16[256,512]{1,0:T(8,128)(2,1)S(1)}, u32[]{:S(2)}, u32[]{:S(2)}) collective-permute-start(bf16[256,512]{1,0:T(8,128)(2,1)} %param.12), channel_id=1, source_target_pairs={{0,0},{33,1},{66,2},{99,3},{132,4},{165,5},{198,6},{231,7},{8,8},{... | collective-permute-start | bytes 786440 | tf_op jit(solution)/shard_map/ppermute | solution.py:44
  16.0 13.4 %collective-permute-start.5 = (bf16[256,1024]{1,0:T(8,128)(2,1)S(1)}, bf16[256,1024]{1,0:T(8,128)(2,1)S(1)}, u32[]{:S(2)}, u32[]{:S(2)}) collective-permute-start(bf16[256,1024]{1,0:T(8,128)(2,1)S(1)} %collective-permute-done.4.s_own), channel_id=1, source_target_pairs={{8,0},{9,1},{10,2},{11,3},{12,4},{13,5},{14,6},{15,7},{0,8},{1,9},... | collective-permute-start | bytes 1572872 | tf_op jit(solution)/shard_map/ppermute | solution.py:44
  20.0 14.5 %collective-permute-start.1 = (bf16[256,1024]{1,0:T(8,128)(2,1)S(1)}, bf16[256,1024]{1,0:T(8,128)(2,1)S(1)}, u32[]{:S(2)}, u32[]{:S(2)}) collective-permute-start(bf16[256,1024]{1,0:T(8,128)(2,1)S(1)} %collective-permute-done.refs_3_), channel_id=1, source_target_pairs={{8,0},{9,1},{10,2},{11,3},{12,4},{13,5},{14,6},{15,7},{0,8},{1,9},... | collective-permute-start | bytes 1572872 | tf_op jit(solution)/shard_map/ppermute | solution.py:44
  20.9 0.7 copy-start.2
  21.5 0.7 copy-start.3
  22.8 1.0 %copy-start = (bf16[256,1024]{1,0:T(8,128)(2,1)S(1)}, bf16[256,1024]{1,0:T(8,128)(2,1)}, u32[]{:S(2)}) copy-start(bf16[256,1024]{1,0:T(8,128)(2,1)} %occ_ref.1) | copy-start | bytes 1572868
  23.8 1.0 %copy-start.1 = (bf16[256,1024]{1,0:T(8,128)(2,1)S(1)}, bf16[256,1024]{1,0:T(8,128)(2,1)}, u32[]{:S(2)}) copy-start(bf16[256,1024]{1,0:T(8,128)(2,1)} %vir_ref.1) | copy-start | bytes 1572868
  26.2 14.4 %collective-permute-start.7 = (bf16[256,512]{1,0:T(8,128)(2,1)S(1)}, bf16[256,512]{1,0:T(8,128)(2,1)S(1)}, u32[]{:S(2)}, u32[]{:S(2)}) collective-permute-start(bf16[256,512]{1,0:T(8,128)(2,1)S(1)} %collective-permute-done.6.s_own), channel_id=1, source_target_pairs={{8,0},{9,1},{10,2},{11,3},{12,4},{13,5},{14,6},{15,7},{0,8},{1,9},... | collective-permute-start | bytes 786440 | tf_op jit(solution)/shard_map/ppermute | solution.py:44
where the time goes:
time: 78.6 us; the launch traced here: 78.1 us
  blocking collectives  35.3 us (45%)
  starting transfers between devices  17.8 us (23%)
  Pallas kernels  15.8 us (20%)
  other arithmetic  4.35 us (6%)
  local copies, waits for them, and re-layouts  3.48 us (4%)
  waiting for transfers between devices  1.23 us (2%)
    all_to_all x1, blocking collectives, per_device(): lax.all_to_all(parts, ('yl', 'yh', 'x'), split_axis=0, concat_axis=0, til...  35.3 us
    ppermute x8, starting transfers between devices, take(): lax.ppermute(array, AXES, [(place(source(*at)), place(at)) for at in ever...  17.8 us
    pallas_call x2, Pallas kernels, chi_term(): pl.pallas_call(kernel, out_shape=jax.ShapeDtypeStruct((2, 2, points, 2 *...  6.07 us
    pallas_call x1, Pallas kernels, occ_term(): pl.pallas_call(occ_kernel, out_shape=jax.ShapeDtypeStruct((2 * points //...  5.13 us
    unnamed x8, local copies, waits for them, and re-layouts  3.39 us
    pallas_call x2, Pallas kernels, scaled(): pl.pallas_call(scale_kernel, out_shape=(shape, shape), in_specs=[VMEM] *...  2.7 us
  transfers between devices with their start and end apart: 8, of which 1 were waited for; matrix products, arithmetic and copies ran while one was open for 5% of the time, Pallas kernels for 19%

commit v1 on v0

--- a/solution.py
+++ b/solution.py
@@ -10,7 +10,7 @@
 
 AXES = ("z", "yl", "c", "yh", "x")
 SIZES = (8, 2, 2, 2, 4)
-NZ, NYL, NC, NYH, NX = SIZES
+_, NYL, NC, NYH, NX = SIZES
 PLANES = (
     (0, 5, 6, 3, 4, 1, 2, 7),
     (1, 3, 7, 5, 2, 0, 4, 6),
@@ -25,6 +25,7 @@
 VMEM = pl.BlockSpec(memory_space=pltpu.VMEM)
 SMEM = pl.BlockSpec(memory_space=pltpu.SMEM)
 MIB = 1024 * 1024
+FIRST_LIMIT = 14 * MIB
 
 
 def place(at):
@@ -93,33 +94,79 @@
     )(occ, vir, occ_decay, vir_decay)
 
 
-def mark_kernel(cos_ref, kept_ref, planes_ref, cos_out, kept_out):
+def plane_of(z, yh, x):
+    found = jnp.int32(0)
+    for g, row in enumerate(PLANES):
+        value = jnp.int32(0)
+        for i, plane in enumerate(row):
+            value = jnp.where(z == i, plane, value)
+        found = jnp.where(yh * NX + x == g, value, found)
+    return found
+
+
+def first_kernel(*refs):
+    sources, outs, held, sems = refs[:8], refs[8:14], refs[14:22], refs[22]
+    copies = [pltpu.make_async_copy(a, b, sems.at[i]) for i, (a, b) in enumerate(zip(sources, held))]
+    for copy in copies:
+        copy.start()
+    for copy in copies:
+        copy.wait()
+    occ_ref, vir_ref, occ_energy, vir_energy, tau_ref, weight_ref, freq_ref, kept_ref = held
+    occ_out, vir_out, occ_decay, vir_decay, cos_out, kept_out = outs
     z, yl, c, yh, x = (lax.axis_index(name) for name in AXES)
     count = kept_ref.shape[0]
     half = kept_out.shape[1] // 2
-    plane = planes_ref[(yh * NX + x) * NZ + z]
+    plane = plane_of(z, yh, x)
     for i, row_yl in enumerate((yl, 1 - yl)):
         row = (z * NYL + row_yl) * NC + c
         for j, from_c in enumerate((c, 1 - c)):
             block = (plane * NYL + yl) * NC + from_c
             kept = kept_ref[(block - row + count) % count].astype(jnp.float32)
             kept_out[i : i + 1, j * half : (j + 1) * half] = jnp.full((1, half), kept, jnp.float32)
-    for i in range(cos_out.shape[0]):
-        cos_out[i : i + 1, :] = jnp.full((1, cos_out.shape[1]), cos_ref[i], jnp.float32)
-
-
-def marked(cosine, kept, planes, points):
-    return pl.pallas_call(
-        mark_kernel,
-        out_shape=(
-            jax.ShapeDtypeStruct((cosine.shape[0], points), jnp.float32),
-            jax.ShapeDtypeStruct((8, 2 * points), jnp.float32),
-        ),
-        in_specs=[SMEM] * 3,
-        out_specs=(VMEM, VMEM),
-        compiler_params=pltpu.CompilerParams(vmem_limit_bytes=2 * MIB),
-        cost_estimate=cost(1e6),
-    )(cosine, kept, planes)
+    taus = tau_ref.shape[0]
+    for k in range(taus):
+        index = jnp.full((1, 128), tau_ref[k].astype(jnp.float32), jnp.float32)
+        time = 0.05 * jnp.exp(index * jnp.float32(math.log(1.5)))
+        wide = jnp.concatenate([time] * (occ_energy.shape[1] // 128), axis=1)
+        occ_decay[k : k + 1, :] = jnp.exp(occ_energy[...] * wide)
+        vir_decay[k : k + 1, :] = jnp.exp(-vir_energy[...] * wide)
+        for w in range(2):
+            cosine = -weight_ref[k] * jnp.cos(freq_ref[w] * time)
+            row = w * taus + k
+            cos_out[row : row + 1, :] = jnp.concatenate([cosine] * (cos_out.shape[1] // 128), axis=1)
+    scale_rows(occ_ref, occ_decay, occ_out)
+    scale_rows(vir_ref, vir_decay, vir_out)
+
+
+def first_term(occ, vir, occ_energies, vir_energies, tau_index, quad_weights, frequencies, distance_kept):
+    taus = tau_index.shape[0]
+    points, states = occ.shape
+    shape = jax.ShapeDtypeStruct((taus, points, states), jnp.bfloat16)
+    decay = jax.ShapeDtypeStruct((taus, states), jnp.float32)
+    rows = jax.ShapeDtypeStruct((2 * taus, points), jnp.float32)
+    marks = jax.ShapeDtypeStruct((8, 2 * points), jnp.float32)
+    operands = (
+        occ,
+        vir,
+        occ_energies.reshape(1, -1),
+        vir_energies.reshape(1, -1),
+        tau_index,
+        quad_weights,
+        frequencies,
+        distance_kept,
+    )
+    operands = tuple(pltpu.with_memory_space_constraint(a, pltpu.HBM) for a in operands)
+    spaces = [pltpu.VMEM] * 4 + [pltpu.SMEM] * 4
+    return pl.pallas_call(
+        first_kernel,
+        out_shape=(shape, shape, decay, decay, rows, marks),
+        in_specs=[pl.BlockSpec(memory_space=pltpu.HBM)] * 8,
+        out_specs=(VMEM,) * 6,
+        scratch_shapes=[space(a.shape, a.dtype) for space, a in zip(spaces, operands)]
+        + [pltpu.SemaphoreType.DMA((8,))],
+        compiler_params=pltpu.CompilerParams(vmem_limit_bytes=FIRST_LIMIT),
+        cost_estimate=cost(1e8),
+    )(*operands)
 
 
 CONTRACT = (((1,), (1,)), ((), ()))
@@ -230,7 +277,6 @@
     frequencies,
     distance_kept,
 ):
-    points = occ_orbitals.shape[0]
     occ_s = from_plane(occ_orbitals)
     occ_near = from_y(occ_orbitals, 1)
     vir_near = from_y(virt_orbitals, -1)
@@ -240,13 +286,16 @@
     vir_t = from_core(vir_s)
     col_t = from_core(col_s)
 
-    times = 0.05 * jnp.exp(tau_index.astype(jnp.float32) * jnp.float32(math.log(1.5)))
-    cosine = (-quad_weights[None, :] * jnp.cos(frequencies[:, None] * times[None, :])).reshape(-1)
-    occ_decay = jnp.exp(occ_energies[None, :] * times[:, None])
-    vir_decay = jnp.exp(-vir_energies[None, :] * times[:, None])
-    planes = jnp.array(PLANES, jnp.int32).reshape(-1)
-    cos_rows, marks = marked(cosine, distance_kept, planes, points)
-    occ_own, vir_own = scaled(occ_orbitals, virt_orbitals, occ_decay, vir_decay)
+    occ_own, vir_own, occ_decay, vir_decay, cos_rows, marks = first_term(
+        occ_orbitals,
+        virt_orbitals,
+        occ_energies,
+        vir_energies,
+        tau_index,
+        quad_weights,
+        frequencies,
+        distance_kept,
+    )
     occ_next, vir_next = scaled(occ_near, vir_near, occ_decay, vir_decay)
     green_occ = occ_term(occ_own, occ_next, occ_s, occ_t)
     chi_own = chi_term(0, cos_rows, marks, vir_own, vir_s, vir_t, green_occ)

time: 78.6 us -> 77 us (0.980)
  waiting for transfers between devices: 1.23 us -> 7.26 us
  other arithmetic: 4.35 us -> 0.81 us
  local copies, waits for them, and re-layouts: 3.48 us -> 0 us
  blocking collectives: 35.3 us -> 33.9 us
  Pallas kernels: 15.8 us -> 16.8 us
    ppermute x8, waiting for transfers between devices: 1.23 us -> 7.26 us  [take(): lax.ppermute(array, AXES, [(place(source(*at)), place(at)) for at in ever...]
    unnamed x8 -> x0, local copies, waits for them, and re-layouts: 3.39 us -> none
    pallas_call x1, Pallas kernels: 0.59 us -> 2.96 us  [first_term(): pl.pallas_call(first_kernel, out_shape=(shape, shape, decay, decay, rows,...]
    mul x2 -> x0, other arithmetic: 1.42 us -> none  [the longest x1 0.76 us: per_device(): -quad_weights[None, :] * jnp.cos(frequencies[:, None] * times[None, :])]
    all_to_all x1, blocking collectives: 35.3 us -> 33.9 us  [per_device(): lax.all_to_all(parts, ('yl', 'yh', 'x'), split_axis=0, concat_axis=0, til...]
    neg x2 -> x0, other arithmetic: 1.35 us -> none  [the longest x1 0.69 us: per_device(): vir_decay = jnp.exp(-vir_energies[None, :] * times[:, None])]
    pallas_call x2 -> x1, Pallas kernels: 2.7 us -> 1.35 us  [scaled(): pl.pallas_call(scale_kernel, out_shape=(shape, shape), in_specs=[VMEM] *...]
  transfers between devices with their start and end apart: 8 -> 8, of which waited for: 1 -> 2; matrix products, arithmetic and copies ran while one was open for 5% -> 0% of each run, Pallas kernels for 19% -> 20%
where the time goes in v1:
time: 77 us; the launch traced here: 76.7 us
  blocking collectives  33.9 us (44%)
  starting transfers between devices  17.8 us (23%)
  Pallas kernels  16.8 us (22%)
  waiting for transfers between devices  7.26 us (9%)
  other arithmetic  0.81 us (1%)
    all_to_all x1, blocking collectives, per_device(): lax.all_to_all(parts, ('yl', 'yh', 'x'), split_axis=0, concat_axis=0, til...  33.9 us
    ppermute x8, starting transfers between devices, take(): lax.ppermute(array, AXES, [(place(source(*at)), place(at)) for at in ever...  17.8 us
    ppermute x8, waiting for transfers between devices, take(): lax.ppermute(array, AXES, [(place(source(*at)), place(at)) for at in ever...  7.26 us
    pallas_call x2, Pallas kernels, chi_term(): pl.pallas_call(kernel, out_shape=jax.ShapeDtypeStruct((2, 2, points, 2 *...  6.07 us
    pallas_call x1, Pallas kernels, occ_term(): pl.pallas_call(occ_kernel, out_shape=jax.ShapeDtypeStruct((2 * points //...  5.14 us
    pallas_call x1, Pallas kernels, first_term(): pl.pallas_call(first_kernel, out_shape=(shape, shape, decay, decay, rows,...  2.96 us
  transfers between devices with their start and end apart: 8, of which 2 were waited for; matrix products, arithmetic and copies ran while one was open for 0% of the time, Pallas kernels for 20%

profile of v1, /device:TPU:1, one launch (start us, length us, event | category | flops | bytes accessed | tf_op | source)
XLA Modules:
  0.0 76.7 jit_solution(8733259700036069)
XLA Ops:
  0.0 1.7 %collective-permute-start.4 = (bf16[256,1024]{1,0:T(8,128)(2,1)}, bf16[256,1024]{1,0:T(8,128)(2,1)S(1)}, u32[]{:S(2)}, u32[]{:S(2)}) collective-permute-start(bf16[256,1024]{1,0:T(8,128)(2,1)} %refs_0_.1), channel_id=1, source_target_pairs={{0,0},{33,1},{66,2},{99,3},{132,4},{165,5},{198,6},{231,7},{8,8},{... | collective-permute-start | bytes 1572872 | tf_op jit(solution)/shard_map/ppermute | solution.py:45
  1.7 1.7 %collective-permute-start = (bf16[256,1024]{1,0:T(8,128)(2,1)}, bf16[256,1024]{1,0:T(8,128)(2,1)S(1)}, u32[]{:S(2)}, u32[]{:S(2)}) collective-permute-start(bf16[256,1024]{1,0:T(8,128)(2,1)} %refs_1_.1), channel_id=1, source_target_pairs={{0,0},{33,1},{66,2},{99,3},{132,4},{165,5},{198,6},{231,7},{8,8},{... | collective-permute-start | bytes 1572872 | tf_op jit(solution)/shard_map/ppermute | solution.py:45
  3.4 11.0 %collective-permute-start.2 = (bf16[256,1024]{1,0:T(8,128)(2,1)}, bf16[256,1024]{1,0:T(8,128)(2,1)S(1)}, u32[]{:S(2)}, u32[]{:S(2)}) collective-permute-start(bf16[256,1024]{1,0:T(8,128)(2,1)} %refs_0_.1), channel_id=1, source_target_pairs={{16,0},{17,1},{18,2},{19,3},{20,4},{21,5},{22,6},{23,7},{24,8},{25... | collective-permute-start | bytes 1572872 | tf_op jit(solution)/shard_map/ppermute | solution.py:45
  14.4 0.0 collective-permute-start.3
  14.4 0.0 collective-permute-done.4.s_own
  14.4 1.2 %collective-permute-start.5 = (bf16[256,1024]{1,0:T(8,128)(2,1)S(1)}, bf16[256,1024]{1,0:T(8,128)(2,1)S(1)}, u32[]{:S(2)}, u32[]{:S(2)}) collective-permute-start(bf16[256,1024]{1,0:T(8,128)(2,1)S(1)} %collective-permute-done.4.s_own), channel_id=1, source_target_pairs={{8,0},{9,1},{10,2},{11,3},{12,4},{13,5},{14,6},{15,7},{0,8},{1,9},... | collective-permute-start | bytes 1572872 | tf_op jit(solution)/shard_map/ppermute | solution.py:45
  15.6 1.6 %collective-permute-start.6 = (bf16[256,512]{1,0:T(8,128)(2,1)}, bf16[256,512]{1,0:T(8,128)(2,1)S(1)}, u32[]{:S(2)}, u32[]{:S(2)}) collective-permute-start(bf16[256,512]{1,0:T(8,128)(2,1)} %param.11), channel_id=1, source_target_pairs={{0,0},{33,1},{66,2},{99,3},{132,4},{165,5},{198,6},{231,7},{8,8},{... | collective-permute-start | bytes 786440 | tf_op jit(solution)/shard_map/ppermute | solution.py:45
  17.2 0.0 collective-permute-done.refs_3_
  17.2 0.0 collective-permute-start.1
  17.2 3.0 %shard_map.91 = (bf16[8,256,1024]{2,1,0:T(8,128)(2,1)S(1)}, bf16[8,256,1024]{2,1,0:T(8,128)(2,1)S(1)}, f32[8,1024]{1,0:T(8,128)S(1)}, f32[8,1024]{1,0:T(8,128)S(...) custom-call(bf16[256,1024]{1,0:T(8,128)(2,1)} %refs_0_.1, bf16[256,1024]{1,0:T(8,128)(2,1)} %refs_1_.1, ...), custom_call_target="tpu_custom_call" | custom-call | flops 100000000 | bytes 4194304 | tf_op jit(solution)/shard_map/pallas_call | solution.py:160
  20.2 0.0 collective-permute-done.6.s_own
  20.2 0.6 collective-permute-start.7
  20.8 4.2 %collective-permute-done.2.occ_ref = bf16[256,1024]{1,0:T(8,128)(2,1)S(1)} collective-permute-done((bf16[256,1024]{1,0:T(8,128)(2,1)}, bf16[256,1024]{1,0:T(8,128)(2,1)S(1)}, u32[]{:S(2)}, u32[]{:S(2)}) %collective-permute-start.2) | collective-permute-done | bytes 524320 | tf_op jit(solution)/shard_map/ppermute | solution.py:45
  25.0 3.0 %collective-permute-done.3.vir_ref = bf16[256,1024]{1,0:T(8,128)(2,1)S(1)} collective-permute-done((bf16[256,1024]{1,0:T(8,128)(2,1)}, bf16[256,1024]{1,0:T(8,128)(2,1)S(1)}, u32[]{:S(2)}, u32[]{:S(2)}) %collective-permute-start.3) | collective-permute-done | bytes 524320 | tf_op jit(solution)/shard_map/ppermute | solution.py:45
  28.0 1.4 %shard_map.92 = (bf16[8,256,1024]{2,1,0:T(8,128)(2,1)S(1)}, bf16[8,256,1024]{2,1,0:T(8,128)(2,1)S(1)}) custom-call(bf16[256,1024]{1,0:T(8,128)(2,1)S(1)} %collective-permute-done.2.occ_ref, bf16[256,1024]{1,0:T(8,128)(2,1)S(1)} %collective-permute-done.3.vir_ref, f32[8,1024]{1,0:T(8,128)S(1)} %get-tuple-element.17.occ_decay_ref, ...), custom_call_target="tpu_custom_call" | custom-call | flops 100000000 | bytes 4194304 | tf_op jit(solution)/shard_map/pallas_call | solution.py:87
  29.4 0.0 collective-permute-done.5.s_other
  29.4 5.1 %shard_map.93.refs_5_ = f32[4,1024,512]{2,1,0:T(8,128)S(1)} custom-call(bf16[8,256,1024]{2,1,0:T(8,128)(2,1)S(1)} %get-tuple-element.16.own_ref, bf16[8,256,1024]{2,1,0:T(8,128)(2,1)S(1)} %get-tuple-element.19.near_ref, bf16[256,1024]{1,0:T(8,128)(2,1)S(1)} %collective-permute-done.4.s_own, bf16[256,1024]{1,0:T(8,128)(2,1)S(1)} %collective-permute-done.5.s_other), custom_call_target="tpu_custom_call" | custom-call | flops 4294967296 | bytes 4194304 | tf_op jit(solution)/shard_map/pallas_call | solution.py:196
  34.5 0.0 collective-permute-done.1.refs_4_
  34.6 3.0 %shard_map.95.near_ref = bf16[2,2,256,512]{3,2,1,0:T(8,128)(2,1)S(1)} custom-call(f32[16,256]{1,0:T(8,128)S(1)} %get-tuple-element.13.refs_0_, f32[8,512]{1,0:T(8,128)S(1)} %get-tuple-element.14.refs_1_, bf16[8,256,1024]{2,1,0:T(8,128)(2,1)S(1)} %get-tuple-element.20.refs_2_, bf16[256,1024]{1,0:T(8,128)(2,1)S(1)} %collective-permute-done.refs_3_, ...), custom_call_target="tpu_custom_call" | custom-call | flops 2147483648 | bytes 4194304 | tf_op jit(solution)/shard_map/pallas_call | solution.py:233
  37.6 3.0 %shard_map.94.own_ref = bf16[2,2,256,512]{3,2,1,0:T(8,128)(2,1)S(1)} custom-call(f32[16,256]{1,0:T(8,128)S(1)} %get-tuple-element.13.refs_0_, f32[8,512]{1,0:T(8,128)S(1)} %get-tuple-element.14.refs_1_, bf16[8,256,1024]{2,1,0:T(8,128)(2,1)S(1)} %get-tuple-element.15.refs_2_, bf16[256,1024]{1,0:T(8,128)(2,1)S(1)} %collective-permute-done.refs_3_, ...), custom_call_target="tpu_custom_call" | custom-call | flops 2147483648 | bytes 4194304 | tf_op jit(solution)/shard_map/pallas_call | solution.py:233
  40.6 0.0 collective-permute-done.7.s_other
  40.7 1.3 %shard_map.96 = bf16[2,8,2,64,256]{4,3,2,1,0:T(8,128)(2,1)S(1)} custom-call(bf16[2,2,256,512]{3,2,1,0:T(8,128)(2,1)S(1)} %shard_map.94.own_ref, bf16[2,2,256,512]{3,2,1,0:T(8,128)(2,1)S(1)} %shard_map.95.near_ref, bf16[256,512]{1,0:T(8,128)(2,1)S(1)} %collective-permute-done.6.s_own, bf16[256,512]{1,0:T(8,128)(2,1)S(1)} %collective-permute-done.7.s_other), custom_call_target="tpu_custom_call" | custom-call | flops 1073741824 | bytes 4194304 | tf_op jit(solution)/shard_map/pallas_call | solution.py:259
  42.0 33.9 %all_to_all.5 = bf16[16,2,64,256]{3,2,1,0:T(8,128)(2,1)S(1)} all-to-all(bf16[16,2,64,256]{3,2,1,0:T(8,128)(2,1)S(1)} %bitcast.3), channel_id=1, replica_groups=mesh['z'=8,'yl'=2,'c'=2,'yh'=2,'x'=4] {'yl','yh','x'}, dimensions={0} | all-to-all | bytes 2097152 | tf_op jit(solution)/shard_map/all_to_all | solution.py:305
  75.9 0.8 %convert_reduce_fusion = f32[2,64,256]{2,1,0:T(8,128)} fusion(bf16[16,2,64,256]{3,2,1,0:T(8,128)(2,1)S(1)} %all_to_all.5), kind=kLoop, calls=%fused_computation | loop fusion | flops 1015808 | bytes 1179648 | tf_op jit(solution)/shard_map/reduce_sum | solution.py:306
Async XLA Ops:
  0.0 14.4 %collective-permute-start.4 = (bf16[256,1024]{1,0:T(8,128)(2,1)}, bf16[256,1024]{1,0:T(8,128)(2,1)S(1)}, u32[]{:S(2)}, u32[]{:S(2)}) collective-permute-start(bf16[256,1024]{1,0:T(8,128)(2,1)} %refs_0_.1), channel_id=1, source_target_pairs={{0,0},{33,1},{66,2},{99,3},{132,4},{165,5},{198,6},{231,7},{8,8},{... | collective-permute-start | bytes 1572872 | tf_op jit(solution)/shard_map/ppermute | solution.py:45
  1.7 15.5 %collective-permute-start = (bf16[256,1024]{1,0:T(8,128)(2,1)}, bf16[256,1024]{1,0:T(8,128)(2,1)S(1)}, u32[]{:S(2)}, u32[]{:S(2)}) collective-permute-start(bf16[256,1024]{1,0:T(8,128)(2,1)} %refs_1_.1), channel_id=1, source_target_pairs={{0,0},{33,1},{66,2},{99,3},{132,4},{165,5},{198,6},{231,7},{8,8},{... | collective-permute-start | bytes 1572872 | tf_op jit(solution)/shard_map/ppermute | solution.py:45
  3.4 21.6 %collective-permute-start.2 = (bf16[256,1024]{1,0:T(8,128)(2,1)}, bf16[256,1024]{1,0:T(8,128)(2,1)S(1)}, u32[]{:S(2)}, u32[]{:S(2)}) collective-permute-start(bf16[256,1024]{1,0:T(8,128)(2,1)} %refs_0_.1), channel_id=1, source_target_pairs={{16,0},{17,1},{18,2},{19,3},{20,4},{21,5},{22,6},{23,7},{24,8},{25... | collective-permute-start | bytes 1572872 | tf_op jit(solution)/shard_map/ppermute | solution.py:45
  14.4 13.7 %collective-permute-start.3 = (bf16[256,1024]{1,0:T(8,128)(2,1)}, bf16[256,1024]{1,0:T(8,128)(2,1)S(1)}, u32[]{:S(2)}, u32[]{:S(2)}) collective-permute-start(bf16[256,1024]{1,0:T(8,128)(2,1)} %refs_1_.1), channel_id=1, source_target_pairs={{20,0},{21,1},{22,2},{23,3},{16,4},{17,5},{18,6},{19,7},{28,8},{29... | collective-permute-start | bytes 1572872 | tf_op jit(solution)/shard_map/ppermute | solution.py:45
  14.4 15.0 %collective-permute-start.5 = (bf16[256,1024]{1,0:T(8,128)(2,1)S(1)}, bf16[256,1024]{1,0:T(8,128)(2,1)S(1)}, u32[]{:S(2)}, u32[]{:S(2)}) collective-permute-start(bf16[256,1024]{1,0:T(8,128)(2,1)S(1)} %collective-permute-done.4.s_own), channel_id=1, source_target_pairs={{8,0},{9,1},{10,2},{11,3},{12,4},{13,5},{14,6},{15,7},{0,8},{1,9},... | collective-permute-start | bytes 1572872 | tf_op jit(solution)/shard_map/ppermute | solution.py:45
  15.6 4.6 %collective-permute-start.6 = (bf16[256,512]{1,0:T(8,128)(2,1)}, bf16[256,512]{1,0:T(8,128)(2,1)S(1)}, u32[]{:S(2)}, u32[]{:S(2)}) collective-permute-start(bf16[256,512]{1,0:T(8,128)(2,1)} %param.11), channel_id=1, source_target_pairs={{0,0},{33,1},{66,2},{99,3},{132,4},{165,5},{198,6},{231,7},{8,8},{... | collective-permute-start | bytes 786440 | tf_op jit(solution)/shard_map/ppermute | solution.py:45
  17.2 17.3 %collective-permute-start.1 = (bf16[256,1024]{1,0:T(8,128)(2,1)S(1)}, bf16[256,1024]{1,0:T(8,128)(2,1)S(1)}, u32[]{:S(2)}, u32[]{:S(2)}) collective-permute-start(bf16[256,1024]{1,0:T(8,128)(2,1)S(1)} %collective-permute-done.refs_3_), channel_id=1, source_target_pairs={{8,0},{9,1},{10,2},{11,3},{12,4},{13,5},{14,6},{15,7},{0,8},{1,9},... | collective-permute-start | bytes 1572872 | tf_op jit(solution)/shard_map/ppermute | solution.py:45
  20.2 20.4 %collective-permute-start.7 = (bf16[256,512]{1,0:T(8,128)(2,1)S(1)}, bf16[256,512]{1,0:T(8,128)(2,1)S(1)}, u32[]{:S(2)}, u32[]{:S(2)}) collective-permute-start(bf16[256,512]{1,0:T(8,128)(2,1)S(1)} %collective-permute-done.6.s_own), channel_id=1, source_target_pairs={{8,0},{9,1},{10,2},{11,3},{12,4},{13,5},{14,6},{15,7},{0,8},{1,9},... | collective-permute-start | bytes 786440 | tf_op jit(solution)/shard_map/ppermute | solution.py:45

commit v2 on v1

--- a/solution.py
+++ b/solution.py
@@ -203,67 +203,87 @@
     )(own, near, s_own, s_other)
 
 
-def chi_kernel(first, row, cos_ref, kept_ref, scaled_ref, s_own, s_other, occ_ref, out_ref):
-    taus, points, _ = scaled_ref.shape
-
-    def body(t):
-        rows = pl.ds(pl.multiple_of(t * TILE, TILE), TILE)
-        for j, s_ref in enumerate((s_own, s_other)):
-            here = slice(j * points, (j + 1) * points)
-            product = green(scaled_ref, t, s_ref) * occ_ref[first + t, :, here]
+def chi_kernel(part, cos_ref, kept_ref, own_ref, near_ref, s_ref, occ_ref, out_ref):
+    taus, points, _ = own_ref.shape
+    tiles = points // TILE
+    here = slice(part * points, (part + 1) * points)
+    for i, source in enumerate((own_ref, near_ref)):
+
+        def body(t, i=i, source=source):
+            rows = pl.ds(pl.multiple_of(i * points + t * TILE, TILE), TILE)
+            product = green(source, t, s_ref) * occ_ref[i * tiles + t, :, here]
             product = product.reshape(taus, TILE, points)
             for w in range(2):
                 chi = cos_ref[w * taus : w * taus + 1, :] * product[0]
                 for k in range(1, taus):
                     chi = chi + cos_ref[w * taus + k : w * taus + k + 1, :] * product[k]
-                chi = chi * kept_ref[row : row + 1, here]
+                chi = chi * kept_ref[i : i + 1, here]
                 high = chi.astype(jnp.bfloat16)
-                out_ref[w, 0, rows, here] = high
-                out_ref[w, 1, rows, here] = (chi - high.astype(jnp.float32)).astype(jnp.bfloat16)
-
-    pl.loop(0, points // TILE)(body)
-
-
-def chi_term(row, cos_rows, marks, vir_scaled, s_own, s_other, green_occ):
-    taus, points, states = vir_scaled.shape
+                out_ref[w, 0, rows, :] = high
+                out_ref[w, 1, rows, :] = (chi - high.astype(jnp.float32)).astype(jnp.bfloat16)
+
+        pl.loop(0, tiles)(body)
+
+
+def chi_term(part, cos_rows, marks, own, near, s, green_occ):
+    taus, points, states = own.shape
 
     def kernel(*refs):
-        chi_kernel(row * (points // TILE), row, *refs)
+        chi_kernel(part, *refs)
 
     return pl.pallas_call(
         kernel,
-        out_shape=jax.ShapeDtypeStruct((2, 2, points, 2 * points), jnp.bfloat16),
+        out_shape=jax.ShapeDtypeStruct((2, 2, 2 * points, points), jnp.bfloat16),
         in_specs=[VMEM] * 6,
         out_specs=VMEM,
         compiler_params=pltpu.CompilerParams(vmem_limit_bytes=24 * MIB),
         cost_estimate=cost(4 * taus * points * points * states),
-    )(cos_rows, marks, vir_scaled, s_own, s_other, green_occ)
-
-
-def answer_kernel(own_ref, near_ref, s_own, s_other, out_ref):
+    )(cos_rows, marks, own, near, s, green_occ)
+
+
+def response_kernel(chi_ref, s_ref, out_ref):
+    points = s_ref.shape[0]
+    for w in range(2):
+        both = chi_ref[w].reshape(4 * points, points)
+        answer = jnp.dot(both, s_ref[...], preferred_element_type=jnp.float32)
+        out_ref[w] = answer[: 2 * points] + answer[2 * points :]
+
+
+def response_term(chi, s):
+    points, columns = s.shape
+    return pl.pallas_call(
+        response_kernel,
+        out_shape=jax.ShapeDtypeStruct((2, 2 * points, columns), jnp.float32),
+        in_specs=[VMEM] * 2,
+        out_specs=VMEM,
+        compiler_params=pltpu.CompilerParams(vmem_limit_bytes=12 * MIB),
+        cost_estimate=cost(16 * points * points * columns),
+    )(chi, s)
+
+
+def answer_kernel(chi_ref, s_ref, carried_ref, out_ref):
     yl = lax.axis_index("yl")
-    points = s_own.shape[0]
+    points = s_ref.shape[0]
     _, groups, _, width, _ = out_ref.shape
-    for slot, chi_ref in ((yl, own_ref), (1 - yl, near_ref)):
-        for w in range(2):
-            both = chi_ref[w].reshape(2 * points, 2 * points)
-            answer = jnp.dot(both[:, :points], s_own[...], preferred_element_type=jnp.float32)
-            answer = answer + jnp.dot(both[:, points:], s_other[...], preferred_element_type=jnp.float32)
-            answer = answer[:points] + answer[points:]
-            out_ref[slot, :, w] = answer.T.astype(jnp.bfloat16).reshape(groups, width, points)
-
-
-def answer_term(own, near, s_own, s_other):
-    points, columns = s_own.shape
+    for w in range(2):
+        both = chi_ref[w].reshape(4 * points, points)
+        answer = jnp.dot(both, s_ref[...], preferred_element_type=jnp.float32)
+        answer = answer[: 2 * points] + answer[2 * points :] + carried_ref[w]
+        for slot, part in ((yl, answer[:points]), (1 - yl, answer[points:])):
+            out_ref[slot, :, w] = part.T.astype(jnp.bfloat16).reshape(groups, width, points)
+
+
+def answer_term(chi, s, carried):
+    points, columns = s.shape
     groups = NYH * NX
     return pl.pallas_call(
         answer_kernel,
         out_shape=jax.ShapeDtypeStruct((NYL, groups, 2, columns // groups, points), jnp.bfloat16),
-        in_specs=[VMEM] * 4,
+        in_specs=[VMEM] * 3,
         out_specs=VMEM,
         compiler_params=pltpu.CompilerParams(vmem_limit_bytes=16 * MIB),
-        cost_estimate=cost(32 * points * points * columns),
-    )(own, near, s_own, s_other)
+        cost_estimate=cost(16 * points * points * columns),
+    )(chi, s, carried)
 
 
 def per_device(
@@ -298,9 +318,10 @@
     )
     occ_next, vir_next = scaled(occ_near, vir_near, occ_decay, vir_decay)
     green_occ = occ_term(occ_own, occ_next, occ_s, occ_t)
-    chi_own = chi_term(0, cos_rows, marks, vir_own, vir_s, vir_t, green_occ)
-    chi_near = chi_term(1, cos_rows, marks, vir_next, vir_s, vir_t, green_occ)
-    parts = answer_term(chi_own, chi_near, col_s, col_t)
+    chi_s = chi_term(0, cos_rows, marks, vir_own, vir_next, vir_s, green_occ)
+    chi_t = chi_term(1, cos_rows, marks, vir_own, vir_next, vir_t, green_occ)
+    carried = response_term(chi_s, col_s)
+    parts = answer_term(chi_t, col_t, carried)
     parts = parts.reshape(-1, *parts.shape[2:])
     spread = lax.all_to_all(parts, ("yl", "yh", "x"), split_axis=0, concat_axis=0, tiled=True)
     return spread.astype(jnp.float32).sum(axis=0)

time: 77 us -> 77.2 us (level)
    pallas_call x2 -> x3, Pallas kernels: 6.07 us -> 6.97 us  [the longest x2 6.27 us: chi_term(): pl.pallas_call(kernel, out_shape=jax.ShapeDtypeStruct((2, 2, 2 * points,...]
  transfers between devices with their start and end apart: 8 -> 8, of which waited for: 2 -> 2; matrix products, arithmetic and copies ran while one was open for 0% -> 0% of each run, Pallas kernels for 20% -> 21%
where the time goes in v2:
time: 77.2 us; the launch traced here: 76.9 us
  blocking collectives  33.7 us (44%)
  starting transfers between devices  17.8 us (23%)
  Pallas kernels  17.2 us (22%)
  waiting for transfers between devices  7.26 us (9%)
  other arithmetic  0.81 us (1%)
    all_to_all x1, blocking collectives, per_device(): lax.all_to_all(parts, ('yl', 'yh', 'x'), split_axis=0, concat_axis=0, til...  33.7 us
    ppermute x8, starting transfers between devices, take(): lax.ppermute(array, AXES, [(place(source(*at)), place(at)) for at in ever...  17.8 us
    ppermute x8, waiting for transfers between devices, take(): lax.ppermute(array, AXES, [(place(source(*at)), place(at)) for at in ever...  7.26 us
    pallas_call x2, Pallas kernels, chi_term(): pl.pallas_call(kernel, out_shape=jax.ShapeDtypeStruct((2, 2, 2 * points,...  6.27 us
    pallas_call x1, Pallas kernels, occ_term(): pl.pallas_call(occ_kernel, out_shape=jax.ShapeDtypeStruct((2 * points //...  5.14 us
    pallas_call x1, Pallas kernels, first_term(): pl.pallas_call(first_kernel, out_shape=(shape, shape, decay, decay, rows,...  2.96 us
  transfers between devices with their start and end apart: 8, of which 2 were waited for; matrix products, arithmetic and copies ran while one was open for 0% of the time, Pallas kernels for 21%

profile of v2, /device:TPU:1, one launch (start us, length us, event | category | flops | bytes accessed | tf_op | source)
XLA Modules:
  0.0 76.9 jit_solution(13879312921920125721)
XLA Ops:
  0.0 1.7 %collective-permute-start.4 = (bf16[256,1024]{1,0:T(8,128)(2,1)}, bf16[256,1024]{1,0:T(8,128)(2,1)S(1)}, u32[]{:S(2)}, u32[]{:S(2)}) collective-permute-start(bf16[256,1024]{1,0:T(8,128)(2,1)} %refs_0_.1), channel_id=1, source_target_pairs={{0,0},{33,1},{66,2},{99,3},{132,4},{165,5},{198,6},{231,7},{8,8},{... | collective-permute-start | bytes 1572872 | tf_op jit(solution)/shard_map/ppermute | solution.py:45
  1.7 1.7 %collective-permute-start.2 = (bf16[256,1024]{1,0:T(8,128)(2,1)}, bf16[256,1024]{1,0:T(8,128)(2,1)S(1)}, u32[]{:S(2)}, u32[]{:S(2)}) collective-permute-start(bf16[256,1024]{1,0:T(8,128)(2,1)} %refs_1_.1), channel_id=1, source_target_pairs={{0,0},{33,1},{66,2},{99,3},{132,4},{165,5},{198,6},{231,7},{8,8},{... | collective-permute-start | bytes 1572872 | tf_op jit(solution)/shard_map/ppermute | solution.py:45
  3.4 11.0 %collective-permute-start = (bf16[256,1024]{1,0:T(8,128)(2,1)}, bf16[256,1024]{1,0:T(8,128)(2,1)S(1)}, u32[]{:S(2)}, u32[]{:S(2)}) collective-permute-start(bf16[256,1024]{1,0:T(8,128)(2,1)} %refs_0_.1), channel_id=1, source_target_pairs={{16,0},{17,1},{18,2},{19,3},{20,4},{21,5},{22,6},{23,7},{24,8},{25... | collective-permute-start | bytes 1572872 | tf_op jit(solution)/shard_map/ppermute | solution.py:45
  14.4 0.0 collective-permute-start.1
  14.4 0.0 collective-permute-done.4.s_own
  14.4 1.2 %collective-permute-start.5 = (bf16[256,1024]{1,0:T(8,128)(2,1)S(1)}, bf16[256,1024]{1,0:T(8,128)(2,1)S(1)}, u32[]{:S(2)}, u32[]{:S(2)}) collective-permute-start(bf16[256,1024]{1,0:T(8,128)(2,1)S(1)} %collective-permute-done.4.s_own), channel_id=1, source_target_pairs={{8,0},{9,1},{10,2},{11,3},{12,4},{13,5},{14,6},{15,7},{0,8},{1,9},... | collective-permute-start | bytes 1572872 | tf_op jit(solution)/shard_map/ppermute | solution.py:45
  15.6 1.6 %collective-permute-start.6 = (bf16[256,512]{1,0:T(8,128)(2,1)}, bf16[256,512]{1,0:T(8,128)(2,1)S(1)}, u32[]{:S(2)}, u32[]{:S(2)}) collective-permute-start(bf16[256,512]{1,0:T(8,128)(2,1)} %param.11), channel_id=1, source_target_pairs={{0,0},{33,1},{66,2},{99,3},{132,4},{165,5},{198,6},{231,7},{8,8},{... | collective-permute-start | bytes 786440 | tf_op jit(solution)/shard_map/ppermute | solution.py:45
  17.2 3.0 %shard_map.91 = (bf16[8,256,1024]{2,1,0:T(8,128)(2,1)S(1)}, bf16[8,256,1024]{2,1,0:T(8,128)(2,1)S(1)}, f32[8,1024]{1,0:T(8,128)S(1)}, f32[8,1024]{1,0:T(8,128)S(...) custom-call(bf16[256,1024]{1,0:T(8,128)(2,1)} %refs_0_.1, bf16[256,1024]{1,0:T(8,128)(2,1)} %refs_1_.1, ...), custom_call_target="tpu_custom_call" | custom-call | flops 100000000 | bytes 4194304 | tf_op jit(solution)/shard_map/pallas_call | solution.py:160
  20.2 0.0 collective-permute-done.6.s_ref
  20.2 0.1 collective-permute-start.7
  20.3 0.0 collective-permute-done.2.refs_4_
  20.3 0.5 collective-permute-start.3
  20.8 4.2 %collective-permute-done.occ_ref = bf16[256,1024]{1,0:T(8,128)(2,1)S(1)} collective-permute-done((bf16[256,1024]{1,0:T(8,128)(2,1)}, bf16[256,1024]{1,0:T(8,128)(2,1)S(1)}, u32[]{:S(2)}, u32[]{:S(2)}) %collective-permute-start) | collective-permute-done | bytes 524320 | tf_op jit(solution)/shard_map/ppermute | solution.py:45
  25.0 3.0 %collective-permute-done.1.vir_ref = bf16[256,1024]{1,0:T(8,128)(2,1)S(1)} collective-permute-done((bf16[256,1024]{1,0:T(8,128)(2,1)}, bf16[256,1024]{1,0:T(8,128)(2,1)S(1)}, u32[]{:S(2)}, u32[]{:S(2)}) %collective-permute-start.1) | collective-permute-done | bytes 524320 | tf_op jit(solution)/shard_map/ppermute | solution.py:45
  28.0 1.4 %shard_map.92 = (bf16[8,256,1024]{2,1,0:T(8,128)(2,1)S(1)}, bf16[8,256,1024]{2,1,0:T(8,128)(2,1)S(1)}) custom-call(bf16[256,1024]{1,0:T(8,128)(2,1)S(1)} %collective-permute-done.occ_ref, bf16[256,1024]{1,0:T(8,128)(2,1)S(1)} %collective-permute-done.1.vir_ref, f32[8,1024]{1,0:T(8,128)S(1)} %get-tuple-element.16.occ_decay_ref, ...), custom_call_target="tpu_custom_call" | custom-call | flops 100000000 | bytes 4194304 | tf_op jit(solution)/shard_map/pallas_call | solution.py:87
  29.4 0.0 collective-permute-done.5.s_other
  29.4 5.1 %shard_map.93.refs_5_ = f32[4,1024,512]{2,1,0:T(8,128)S(1)} custom-call(bf16[8,256,1024]{2,1,0:T(8,128)(2,1)S(1)} %get-tuple-element.19.own_ref, bf16[8,256,1024]{2,1,0:T(8,128)(2,1)S(1)} %get-tuple-element.20.near_ref, bf16[256,1024]{1,0:T(8,128)(2,1)S(1)} %collective-permute-done.4.s_own, bf16[256,1024]{1,0:T(8,128)(2,1)S(1)} %collective-permute-done.5.s_other), custom_call_target="tpu_custom_call" | custom-call | flops 4294967296 | bytes 4194304 | tf_op jit(solution)/shard_map/pallas_call | solution.py:196
  34.5 3.1 %shard_map.95.chi_ref = bf16[2,2,512,256]{3,2,1,0:T(8,128)(2,1)S(1)} custom-call(f32[16,256]{1,0:T(8,128)S(1)} %get-tuple-element.13.refs_0_, f32[8,512]{1,0:T(8,128)S(1)} %get-tuple-element.14.refs_1_, bf16[8,256,1024]{2,1,0:T(8,128)(2,1)S(1)} %get-tuple-element.15.refs_2_, bf16[8,256,1024]{2,1,0:T(8,128)(2,1)S(1)} %get-tuple-element.18.refs_3_, ...), custom_call_target="tpu_custom_call" | custom-call | flops 2147483648 | bytes 4194304 | tf_op jit(solution)/shard_map/pallas_call | solution.py:234
  37.7 0.7 shard_map.96.carried_ref
  38.4 0.0 collective-permute-done.3.refs_4_
  38.4 3.1 %shard_map.94.chi_ref = bf16[2,2,512,256]{3,2,1,0:T(8,128)(2,1)S(1)} custom-call(f32[16,256]{1,0:T(8,128)S(1)} %get-tuple-element.13.refs_0_, f32[8,512]{1,0:T(8,128)S(1)} %get-tuple-element.14.refs_1_, bf16[8,256,1024]{2,1,0:T(8,128)(2,1)S(1)} %get-tuple-element.15.refs_2_, bf16[8,256,1024]{2,1,0:T(8,128)(2,1)S(1)} %get-tuple-element.18.refs_3_, ...), custom_call_target="tpu_custom_call" | custom-call | flops 2147483648 | bytes 4194304 | tf_op jit(solution)/shard_map/pallas_call | solution.py:234
  41.6 0.0 collective-permute-done.7.s_ref
  41.6 0.8 %shard_map.97 = bf16[2,8,2,64,256]{4,3,2,1,0:T(8,128)(2,1)S(1)} custom-call(bf16[2,2,512,256]{3,2,1,0:T(8,128)(2,1)S(1)} %shard_map.94.chi_ref, bf16[256,512]{1,0:T(8,128)(2,1)S(1)} %collective-permute-done.7.s_ref, f32[2,512,512]{2,1,0:T(8,128)S(1)} %shard_map.96.carried_ref), custom_call_target="tpu_custom_call" | custom-call | flops 536870912 | bytes 4194304 | tf_op jit(solution)/shard_map/pallas_call | solution.py:279
  42.3 33.7 %all_to_all.5 = bf16[16,2,64,256]{3,2,1,0:T(8,128)(2,1)S(1)} all-to-all(bf16[16,2,64,256]{3,2,1,0:T(8,128)(2,1)S(1)} %bitcast.3), channel_id=1, replica_groups=mesh['z'=8,'yl'=2,'c'=2,'yh'=2,'x'=4] {'yl','yh','x'}, dimensions={0} | all-to-all | bytes 2097152 | tf_op jit(solution)/shard_map/all_to_all | solution.py:326
  76.1 0.8 %convert_reduce_fusion = f32[2,64,256]{2,1,0:T(8,128)} fusion(bf16[16,2,64,256]{3,2,1,0:T(8,128)(2,1)S(1)} %all_to_all.5), kind=kLoop, calls=%fused_computation | loop fusion | flops 1015808 | bytes 1179648 | tf_op jit(solution)/shard_map/reduce_sum | solution.py:327
Async XLA Ops:
  0.0 14.4 %collective-permute-start.4 = (bf16[256,1024]{1,0:T(8,128)(2,1)}, bf16[256,1024]{1,0:T(8,128)(2,1)S(1)}, u32[]{:S(2)}, u32[]{:S(2)}) collective-permute-start(bf16[256,1024]{1,0:T(8,128)(2,1)} %refs_0_.1), channel_id=1, source_target_pairs={{0,0},{33,1},{66,2},{99,3},{132,4},{165,5},{198,6},{231,7},{8,8},{... | collective-permute-start | bytes 1572872 | tf_op jit(solution)/shard_map/ppermute | solution.py:45
  1.7 18.6 %collective-permute-start.2 = (bf16[256,1024]{1,0:T(8,128)(2,1)}, bf16[256,1024]{1,0:T(8,128)(2,1)S(1)}, u32[]{:S(2)}, u32[]{:S(2)}) collective-permute-start(bf16[256,1024]{1,0:T(8,128)(2,1)} %refs_1_.1), channel_id=1, source_target_pairs={{0,0},{33,1},{66,2},{99,3},{132,4},{165,5},{198,6},{231,7},{8,8},{... | collective-permute-start | bytes 1572872 | tf_op jit(solution)/shard_map/ppermute | solution.py:45
  3.4 21.6 %collective-permute-start = (bf16[256,1024]{1,0:T(8,128)(2,1)}, bf16[256,1024]{1,0:T(8,128)(2,1)S(1)}, u32[]{:S(2)}, u32[]{:S(2)}) collective-permute-start(bf16[256,1024]{1,0:T(8,128)(2,1)} %refs_0_.1), channel_id=1, source_target_pairs={{16,0},{17,1},{18,2},{19,3},{20,4},{21,5},{22,6},{23,7},{24,8},{25... | collective-permute-start | bytes 1572872 | tf_op jit(solution)/shard_map/ppermute | solution.py:45
  14.4 13.7 %collective-permute-start.1 = (bf16[256,1024]{1,0:T(8,128)(2,1)}, bf16[256,1024]{1,0:T(8,128)(2,1)S(1)}, u32[]{:S(2)}, u32[]{:S(2)}) collective-permute-start(bf16[256,1024]{1,0:T(8,128)(2,1)} %refs_1_.1), channel_id=1, source_target_pairs={{20,0},{21,1},{22,2},{23,3},{16,4},{17,5},{18,6},{19,7},{28,8},{29... | collective-permute-start | bytes 1572872 | tf_op jit(solution)/shard_map/ppermute | solution.py:45
  14.4 15.0 %collective-permute-start.5 = (bf16[256,1024]{1,0:T(8,128)(2,1)S(1)}, bf16[256,1024]{1,0:T(8,128)(2,1)S(1)}, u32[]{:S(2)}, u32[]{:S(2)}) collective-permute-start(bf16[256,1024]{1,0:T(8,128)(2,1)S(1)} %collective-permute-done.4.s_own), channel_id=1, source_target_pairs={{8,0},{9,1},{10,2},{11,3},{12,4},{13,5},{14,6},{15,7},{0,8},{1,9},... | collective-permute-start | bytes 1572872 | tf_op jit(solution)/shard_map/ppermute | solution.py:45
  15.6 4.6 %collective-permute-start.6 = (bf16[256,512]{1,0:T(8,128)(2,1)}, bf16[256,512]{1,0:T(8,128)(2,1)S(1)}, u32[]{:S(2)}, u32[]{:S(2)}) collective-permute-start(bf16[256,512]{1,0:T(8,128)(2,1)} %param.11), channel_id=1, source_target_pairs={{0,0},{33,1},{66,2},{99,3},{132,4},{165,5},{198,6},{231,7},{8,8},{... | collective-permute-start | bytes 786440 | tf_op jit(solution)/shard_map/ppermute | solution.py:45
  20.2 21.4 %collective-permute-start.7 = (bf16[256,512]{1,0:T(8,128)(2,1)S(1)}, bf16[256,512]{1,0:T(8,128)(2,1)S(1)}, u32[]{:S(2)}, u32[]{:S(2)}) collective-permute-start(bf16[256,512]{1,0:T(8,128)(2,1)S(1)} %collective-permute-done.6.s_ref), channel_id=1, source_target_pairs={{8,0},{9,1},{10,2},{11,3},{12,4},{13,5},{14,6},{15,7},{0,8},{1,9},... | collective-permute-start | bytes 786440 | tf_op jit(solution)/shard_map/ppermute | solution.py:45
  20.3 18.1 %collective-permute-start.3 = (bf16[256,1024]{1,0:T(8,128)(2,1)S(1)}, bf16[256,1024]{1,0:T(8,128)(2,1)S(1)}, u32[]{:S(2)}, u32[]{:S(2)}) collective-permute-start(bf16[256,1024]{1,0:T(8,128)(2,1)S(1)} %collective-permute-done.2.refs_4_), channel_id=1, source_target_pairs={{8,0},{9,1},{10,2},{11,3},{12,4},{13,5},{14,6},{15,7},{0,8},{1,9},... | collective-permute-start | bytes 1572872 | tf_op jit(solution)/shard_map/ppermute | solution.py:45

commit v3 on v2

--- a/solution.py
+++ b/solution.py
@@ -25,7 +25,6 @@
 VMEM = pl.BlockSpec(memory_space=pltpu.VMEM)
 SMEM = pl.BlockSpec(memory_space=pltpu.SMEM)
 MIB = 1024 * 1024
-FIRST_LIMIT = 14 * MIB
 
 
 def place(at):
@@ -77,21 +76,21 @@
     pl.loop(0, source.shape[0] // step)(body)
 
 
-def scale_kernel(occ_ref, vir_ref, occ_decay_ref, vir_decay_ref, occ_out, vir_out):
-    scale_rows(occ_ref, occ_decay_ref, occ_out)
-    scale_rows(vir_ref, vir_decay_ref, vir_out)
-
-
-def scaled(occ, vir, occ_decay, vir_decay):
-    shape = jax.ShapeDtypeStruct((occ_decay.shape[0], *occ.shape), jnp.bfloat16)
+def scale_kernel(decay_ref, *refs):
+    half = len(refs) // 2
+    for source, out in zip(refs[:half], refs[half:]):
+        scale_rows(source, decay_ref, out)
+
+
+def scaled(decay, *arrays):
     return pl.pallas_call(
         scale_kernel,
-        out_shape=(shape, shape),
-        in_specs=[VMEM] * 4,
-        out_specs=(VMEM, VMEM),
+        out_shape=[jax.ShapeDtypeStruct((decay.shape[0], *a.shape), jnp.bfloat16) for a in arrays],
+        in_specs=[VMEM] * (1 + len(arrays)),
+        out_specs=[VMEM] * len(arrays),
         compiler_params=pltpu.CompilerParams(vmem_limit_bytes=12 * MIB),
         cost_estimate=cost(1e8),
-    )(occ, vir, occ_decay, vir_decay)
+    )(decay, *arrays)
 
 
 def plane_of(z, yh, x):
@@ -105,14 +104,15 @@
 
 
 def first_kernel(*refs):
-    sources, outs, held, sems = refs[:8], refs[8:14], refs[14:22], refs[22]
+    sources, outs, held, sems = refs[:8], refs[8:14], refs[14:21], refs[21]
+    held = (*held, outs[-1])
     copies = [pltpu.make_async_copy(a, b, sems.at[i]) for i, (a, b) in enumerate(zip(sources, held))]
     for copy in copies:
         copy.start()
     for copy in copies:
         copy.wait()
-    occ_ref, vir_ref, occ_energy, vir_energy, tau_ref, weight_ref, freq_ref, kept_ref = held
-    occ_out, vir_out, occ_decay, vir_decay, cos_out, kept_out = outs
+    occ_ref, occ_energy, vir_energy, tau_ref, weight_ref, freq_ref, kept_ref, _ = held
+    occ_out, occ_decay, vir_decay, cos_out, kept_out, _ = outs
     z, yl, c, yh, x = (lax.axis_index(name) for name in AXES)
     count = kept_ref.shape[0]
     half = kept_out.shape[1] // 2
@@ -135,36 +135,39 @@
             row = w * taus + k
             cos_out[row : row + 1, :] = jnp.concatenate([cosine] * (cos_out.shape[1] // 128), axis=1)
     scale_rows(occ_ref, occ_decay, occ_out)
-    scale_rows(vir_ref, vir_decay, vir_out)
 
 
 def first_term(occ, vir, occ_energies, vir_energies, tau_index, quad_weights, frequencies, distance_kept):
     taus = tau_index.shape[0]
     points, states = occ.shape
-    shape = jax.ShapeDtypeStruct((taus, points, states), jnp.bfloat16)
     decay = jax.ShapeDtypeStruct((taus, states), jnp.float32)
-    rows = jax.ShapeDtypeStruct((2 * taus, points), jnp.float32)
-    marks = jax.ShapeDtypeStruct((8, 2 * points), jnp.float32)
     operands = (
         occ,
-        vir,
         occ_energies.reshape(1, -1),
         vir_energies.reshape(1, -1),
         tau_index,
         quad_weights,
         frequencies,
         distance_kept,
+        vir,
     )
     operands = tuple(pltpu.with_memory_space_constraint(a, pltpu.HBM) for a in operands)
-    spaces = [pltpu.VMEM] * 4 + [pltpu.SMEM] * 4
+    spaces = [pltpu.VMEM] * 3 + [pltpu.SMEM] * 4
     return pl.pallas_call(
         first_kernel,
-        out_shape=(shape, shape, decay, decay, rows, marks),
+        out_shape=(
+            jax.ShapeDtypeStruct((taus, points, states), jnp.bfloat16),
+            decay,
+            decay,
+            jax.ShapeDtypeStruct((2 * taus, points), jnp.float32),
+            jax.ShapeDtypeStruct((8, 2 * points), jnp.float32),
+            jax.ShapeDtypeStruct(vir.shape, vir.dtype),
+        ),
         in_specs=[pl.BlockSpec(memory_space=pltpu.HBM)] * 8,
         out_specs=(VMEM,) * 6,
         scratch_shapes=[space(a.shape, a.dtype) for space, a in zip(spaces, operands)]
         + [pltpu.SemaphoreType.DMA((8,))],
-        compiler_params=pltpu.CompilerParams(vmem_limit_bytes=FIRST_LIMIT),
+        compiler_params=pltpu.CompilerParams(vmem_limit_bytes=14 * MIB),
         cost_estimate=cost(1e8),
     )(*operands)
 
@@ -174,7 +177,7 @@
 
 def green(scaled_ref, tile, s_ref):
     taus, _, states = scaled_ref.shape
-    rows = pl.ds(pl.multiple_of(tile * TILE, TILE), TILE)
+    rows = pl.ds(tile * TILE, TILE)
     left = scaled_ref[:, rows, :].reshape(taus * TILE, states)
     return lax.dot_general(left, s_ref[...], CONTRACT, preferred_element_type=jnp.float32)
 
@@ -188,7 +191,8 @@
             for j, s_ref in enumerate((s_own, s_other)):
                 out_ref[i * tiles + t, :, j * points : (j + 1) * points] = green(source, t, s_ref)
 
-        pl.loop(0, tiles)(body)
+        for t in range(tiles):
+            body(t)
 
 
 def occ_term(own, near, s_own, s_other):
@@ -210,7 +214,7 @@
     for i, source in enumerate((own_ref, near_ref)):
 
         def body(t, i=i, source=source):
-            rows = pl.ds(pl.multiple_of(i * points + t * TILE, TILE), TILE)
+            rows = pl.ds(i * points + t * TILE, TILE)
             product = green(source, t, s_ref) * occ_ref[i * tiles + t, :, here]
             product = product.reshape(taus, TILE, points)
             for w in range(2):
@@ -222,7 +226,8 @@
                 out_ref[w, 0, rows, :] = high
                 out_ref[w, 1, rows, :] = (chi - high.astype(jnp.float32)).astype(jnp.bfloat16)
 
-        pl.loop(0, tiles)(body)
+        for t in range(tiles):
+            body(t)
 
 
 def chi_term(part, cos_rows, marks, own, near, s, green_occ):
@@ -241,49 +246,31 @@
     )(cos_rows, marks, own, near, s, green_occ)
 
 
-def response_kernel(chi_ref, s_ref, out_ref):
-    points = s_ref.shape[0]
-    for w in range(2):
-        both = chi_ref[w].reshape(4 * points, points)
-        answer = jnp.dot(both, s_ref[...], preferred_element_type=jnp.float32)
-        out_ref[w] = answer[: 2 * points] + answer[2 * points :]
-
-
-def response_term(chi, s):
-    points, columns = s.shape
-    return pl.pallas_call(
-        response_kernel,
-        out_shape=jax.ShapeDtypeStruct((2, 2 * points, columns), jnp.float32),
-        in_specs=[VMEM] * 2,
-        out_specs=VMEM,
-        compiler_params=pltpu.CompilerParams(vmem_limit_bytes=12 * MIB),
-        cost_estimate=cost(16 * points * points * columns),
-    )(chi, s)
-
-
-def answer_kernel(chi_ref, s_ref, carried_ref, out_ref):
+def answer_kernel(chi_ref, chi_other, s_ref, s_other, out_ref):
     yl = lax.axis_index("yl")
     points = s_ref.shape[0]
     _, groups, _, width, _ = out_ref.shape
     for w in range(2):
         both = chi_ref[w].reshape(4 * points, points)
         answer = jnp.dot(both, s_ref[...], preferred_element_type=jnp.float32)
-        answer = answer[: 2 * points] + answer[2 * points :] + carried_ref[w]
+        both = chi_other[w].reshape(4 * points, points)
+        answer = answer + jnp.dot(both, s_other[...], preferred_element_type=jnp.float32)
+        answer = answer[: 2 * points] + answer[2 * points :]
         for slot, part in ((yl, answer[:points]), (1 - yl, answer[points:])):
             out_ref[slot, :, w] = part.T.astype(jnp.bfloat16).reshape(groups, width, points)
 
 
-def answer_term(chi, s, carried):
+def answer_term(chi, chi_other, s, s_other):
     points, columns = s.shape
     groups = NYH * NX
     return pl.pallas_call(
         answer_kernel,
         out_shape=jax.ShapeDtypeStruct((NYL, groups, 2, columns // groups, points), jnp.bfloat16),
-        in_specs=[VMEM] * 3,
+        in_specs=[VMEM] * 4,
         out_specs=VMEM,
         compiler_params=pltpu.CompilerParams(vmem_limit_bytes=16 * MIB),
-        cost_estimate=cost(16 * points * points * columns),
-    )(chi, s, carried)
+        cost_estimate=cost(32 * points * points * columns),
+    )(chi, chi_other, s, s_other)
 
 
 def per_device(
@@ -306,7 +293,7 @@
     vir_t = from_core(vir_s)
     col_t = from_core(col_s)
 
-    occ_own, vir_own, occ_decay, vir_decay, cos_rows, marks = first_term(
+    occ_own, occ_decay, vir_decay, cos_rows, marks, vir_held = first_term(
         occ_orbitals,
         virt_orbitals,
         occ_energies,
@@ -316,12 +303,13 @@
         frequencies,
         distance_kept,
     )
-    occ_next, vir_next = scaled(occ_near, vir_near, occ_decay, vir_decay)
+    (occ_next,) = scaled(occ_decay, occ_near)
     green_occ = occ_term(occ_own, occ_next, occ_s, occ_t)
+    vir_near, green_occ = lax.optimization_barrier((vir_near, green_occ))
+    vir_own, vir_next = scaled(vir_decay, vir_held, vir_near)
     chi_s = chi_term(0, cos_rows, marks, vir_own, vir_next, vir_s, green_occ)
     chi_t = chi_term(1, cos_rows, marks, vir_own, vir_next, vir_t, green_occ)
-    carried = response_term(chi_s, col_s)
-    parts = answer_term(chi_t, col_t, carried)
+    parts = answer_term(chi_s, chi_t, col_s, col_t)
     parts = parts.reshape(-1, *parts.shape[2:])
     spread = lax.all_to_all(parts, ("yl", "yh", "x"), split_axis=0, concat_axis=0, tiled=True)
     return spread.astype(jnp.float32).sum(axis=0)

time: 77.2 us -> 76.6 us (level)
  waiting for transfers between devices: 7.26 us -> 20.8 us
  blocking collectives: 33.7 us -> 20.9 us
  Pallas kernels: 17.2 us -> 15.9 us
    ppermute x8, waiting for transfers between devices: 7.26 us -> 20.8 us  [take(): lax.ppermute(array, AXES, [(place(source(*at)), place(at)) for at in ever...]
    all_to_all x1, blocking collectives: 33.7 us -> 20.9 us  [per_device(): lax.all_to_all(parts, ('yl', 'yh', 'x'), split_axis=0, concat_axis=0, til...]
  transfers between devices with their start and end apart: 8 -> 8, of which waited for: 2 -> 2; matrix products, arithmetic and copies ran while one was open for 0% -> 0% of each run, Pallas kernels for 21% -> 19%
where the time goes in v3:
time: 76.6 us; the launch traced here: 76.3 us
  blocking collectives  20.9 us (27%)
  waiting for transfers between devices  20.8 us (27%)
  starting transfers between devices  17.8 us (23%)
  Pallas kernels  15.9 us (21%)
  other arithmetic  0.81 us (1%)
    all_to_all x1, blocking collectives, per_device(): lax.all_to_all(parts, ('yl', 'yh', 'x'), split_axis=0, concat_axis=0, til...  20.9 us
    ppermute x8, waiting for transfers between devices, take(): lax.ppermute(array, AXES, [(place(source(*at)), place(at)) for at in ever...  20.8 us
    ppermute x8, starting transfers between devices, take(): lax.ppermute(array, AXES, [(place(source(*at)), place(at)) for at in ever...  17.8 us
    pallas_call x2, Pallas kernels, chi_term(): pl.pallas_call(kernel, out_shape=jax.ShapeDtypeStruct((2, 2, 2 * points,...  5.79 us
    pallas_call x1, Pallas kernels, occ_term(): pl.pallas_call(occ_kernel, out_shape=jax.ShapeDtypeStruct((2 * points //...  4.53 us
    pallas_call x1, Pallas kernels, first_term(): pl.pallas_call(first_kernel, out_shape=(jax.ShapeDtypeStruct((taus, point...  2.26 us
    pallas_call x2, Pallas kernels, scaled(): pl.pallas_call(scale_kernel, out_shape=[jax.ShapeDtypeStruct((decay.shape...  2.03 us
  transfers between devices with their start and end apart: 8, of which 2 were waited for; matrix products, arithmetic and copies ran while one was open for 0% of the time, Pallas kernels for 19%

profile of v3, /device:TPU:1, one launch (start us, length us, event | category | flops | bytes accessed | tf_op | source)
XLA Modules:
  0.0 76.3 jit_solution(15022612443336965140)
XLA Ops:
  0.0 1.7 %collective-permute-start.2 = (bf16[256,1024]{1,0:T(8,128)(2,1)}, bf16[256,1024]{1,0:T(8,128)(2,1)S(1)}, u32[]{:S(2)}, u32[]{:S(2)}) collective-permute-start(bf16[256,1024]{1,0:T(8,128)(2,1)} %refs_0_.1), channel_id=1, source_target_pairs={{0,0},{33,1},{66,2},{99,3},{132,4},{165,5},{198,6},{231,7},{8,8},{... | collective-permute-start | bytes 1572872 | tf_op jit(solution)/shard_map/ppermute | solution.py:44
  1.7 1.7 %collective-permute-start.4 = (bf16[256,1024]{1,0:T(8,128)(2,1)}, bf16[256,1024]{1,0:T(8,128)(2,1)S(1)}, u32[]{:S(2)}, u32[]{:S(2)}) collective-permute-start(bf16[256,1024]{1,0:T(8,128)(2,1)} %refs_7_.1), channel_id=1, source_target_pairs={{0,0},{33,1},{66,2},{99,3},{132,4},{165,5},{198,6},{231,7},{8,8},{... | collective-permute-start | bytes 1572872 | tf_op jit(solution)/shard_map/ppermute | solution.py:44
  3.4 11.0 %collective-permute-start.1 = (bf16[256,1024]{1,0:T(8,128)(2,1)}, bf16[256,1024]{1,0:T(8,128)(2,1)S(1)}, u32[]{:S(2)}, u32[]{:S(2)}) collective-permute-start(bf16[256,1024]{1,0:T(8,128)(2,1)} %refs_0_.1), channel_id=1, source_target_pairs={{16,0},{17,1},{18,2},{19,3},{20,4},{21,5},{22,6},{23,7},{24,8},{25... | collective-permute-start | bytes 1572872 | tf_op jit(solution)/shard_map/ppermute | solution.py:44
  14.4 0.0 collective-permute-done.2.s_own
  14.4 1.2 %collective-permute-start.3 = (bf16[256,1024]{1,0:T(8,128)(2,1)S(1)}, bf16[256,1024]{1,0:T(8,128)(2,1)S(1)}, u32[]{:S(2)}, u32[]{:S(2)}) collective-permute-start(bf16[256,1024]{1,0:T(8,128)(2,1)S(1)} %collective-permute-done.2.s_own), channel_id=1, source_target_pairs={{8,0},{9,1},{10,2},{11,3},{12,4},{13,5},{14,6},{15,7},{0,8},{1,9},... | collective-permute-start | bytes 1572872 | tf_op jit(solution)/shard_map/ppermute | solution.py:44
  15.6 1.6 %collective-permute-start.6 = (bf16[256,512]{1,0:T(8,128)(2,1)}, bf16[256,512]{1,0:T(8,128)(2,1)S(1)}, u32[]{:S(2)}, u32[]{:S(2)}) collective-permute-start(bf16[256,512]{1,0:T(8,128)(2,1)} %param.11), channel_id=1, source_target_pairs={{0,0},{33,1},{66,2},{99,3},{132,4},{165,5},{198,6},{231,7},{8,8},{... | collective-permute-start | bytes 786440 | tf_op jit(solution)/shard_map/ppermute | solution.py:44
  17.2 0.0 collective-permute-start
  17.2 2.3 %shard_map.91 = (bf16[8,256,1024]{2,1,0:T(8,128)(2,1)S(1)}, f32[8,1024]{1,0:T(8,128)S(1)}, f32[8,1024]{1,0:T(8,128)S(1)}, f32[16,256]{1,0:T(8,128)S(1)}, f32[8,5...) custom-call(bf16[256,1024]{1,0:T(8,128)(2,1)} %refs_0_.1, f32[1,1024]{1,0:T(1,128)} %bitcast.4, f32[1,1024]{1,0:T(1,128)} %bitcast.5, ...), custom_call_target="tpu_custom_call" | custom-call | flops 100000000 | bytes 4194304 | tf_op jit(solution)/shard_map/pallas_call | solution.py:156
  19.5 0.0 collective-permute-done.6.s_ref
  19.5 0.1 collective-permute-start.7
  19.6 0.0 collective-permute-done.4.refs_4_
  19.6 0.5 collective-permute-start.5
  20.1 4.9 %collective-permute-done.1.refs_0_ = bf16[256,1024]{1,0:T(8,128)(2,1)S(1)} collective-permute-done((bf16[256,1024]{1,0:T(8,128)(2,1)}, bf16[256,1024]{1,0:T(8,128)(2,1)S(1)}, u32[]{:S(2)}, u32[]{:S(2)}) %collective-permute-start.1) | collective-permute-done | bytes 524320 | tf_op jit(solution)/shard_map/ppermute | solution.py:44
  25.0 0.7 shard_map.92.near_ref
  25.7 0.0 collective-permute-done.3.s_other
  25.7 4.5 %shard_map.93.refs_5_ = f32[4,1024,512]{2,1,0:T(8,128)S(1)} custom-call(bf16[8,256,1024]{2,1,0:T(8,128)(2,1)S(1)} %get-tuple-element.19.own_ref, bf16[8,256,1024]{2,1,0:T(8,128)(2,1)S(1)} %shard_map.92.near_ref, bf16[256,1024]{1,0:T(8,128)(2,1)S(1)} %collective-permute-done.2.s_own, bf16[256,1024]{1,0:T(8,128)(2,1)S(1)} %collective-permute-done.3.s_other), custom_call_target="tpu_custom_call" | custom-call | flops 4294967296 | bytes 4194304 | tf_op jit(solution)/shard_map/pallas_call | solution.py:200
  30.2 15.9 %collective-permute-done.refs_1_ = bf16[256,1024]{1,0:T(8,128)(2,1)S(1)} collective-permute-done((bf16[256,1024]{1,0:T(8,128)(2,1)}, bf16[256,1024]{1,0:T(8,128)(2,1)S(1)}, u32[]{:S(2)}, u32[]{:S(2)}) %collective-permute-start) | collective-permute-done | bytes 524320 | tf_op jit(solution)/shard_map/ppermute | solution.py:44
  46.1 1.4 %shard_map.94 = (bf16[8,256,1024]{2,1,0:T(8,128)(2,1)S(1)}, bf16[8,256,1024]{2,1,0:T(8,128)(2,1)S(1)}) custom-call(f32[8,1024]{1,0:T(8,128)S(1)} %get-tuple-element.17.decay_ref, bf16[256,1024]{1,0:T(8,128)(2,1)S(1)} %get-tuple-element.18.refs_0_, bf16[256,1024]{1,0:T(8,128)(2,1)S(1)} %collective-permute-done.refs_1_), custom_call_target="tpu_custom_call" | custom-call | flops 100000000 | bytes 4194304 | tf_op jit(solution)/shard_map/pallas_call | solution.py:86
  47.5 2.9 %shard_map.95.chi_ref = bf16[2,2,512,256]{3,2,1,0:T(8,128)(2,1)S(1)} custom-call(f32[16,256]{1,0:T(8,128)S(1)} %get-tuple-element.15.refs_0_, f32[8,512]{1,0:T(8,128)S(1)} %get-tuple-element.16.refs_1_, bf16[8,256,1024]{2,1,0:T(8,128)(2,1)S(1)} %get-tuple-element.22.refs_2_, bf16[8,256,1024]{2,1,0:T(8,128)(2,1)S(1)} %get-tuple-element.23.refs_3_, ...), custom_call_target="tpu_custom_call" | custom-call | flops 2147483648 | bytes 4194304 | tf_op jit(solution)/shard_map/pallas_call | solution.py:239
  50.4 0.0 collective-permute-done.5.refs_4_
  50.4 2.9 %shard_map.96.chi_other = bf16[2,2,512,256]{3,2,1,0:T(8,128)(2,1)S(1)} custom-call(f32[16,256]{1,0:T(8,128)S(1)} %get-tuple-element.15.refs_0_, f32[8,512]{1,0:T(8,128)S(1)} %get-tuple-element.16.refs_1_, bf16[8,256,1024]{2,1,0:T(8,128)(2,1)S(1)} %get-tuple-element.22.refs_2_, bf16[8,256,1024]{2,1,0:T(8,128)(2,1)S(1)} %get-tuple-element.23.refs_3_, ...), custom_call_target="tpu_custom_call" | custom-call | flops 2147483648 | bytes 4194304 | tf_op jit(solution)/shard_map/pallas_call | solution.py:239
  53.3 0.0 collective-permute-done.7.s_other
  53.3 1.3 %shard_map.97 = bf16[2,8,2,64,256]{4,3,2,1,0:T(8,128)(2,1)S(1)} custom-call(bf16[2,2,512,256]{3,2,1,0:T(8,128)(2,1)S(1)} %shard_map.95.chi_ref, bf16[2,2,512,256]{3,2,1,0:T(8,128)(2,1)S(1)} %shard_map.96.chi_other, bf16[256,512]{1,0:T(8,128)(2,1)S(1)} %collective-permute-done.6.s_ref, bf16[256,512]{1,0:T(8,128)(2,1)S(1)} %collective-permute-done.7.s_other), custom_call_target="tpu_custom_call" | custom-call | flops 1073741824 | bytes 4194304 | tf_op jit(solution)/shard_map/pallas_call | solution.py:266
  54.6 20.9 %all_to_all.5 = bf16[16,2,64,256]{3,2,1,0:T(8,128)(2,1)S(1)} all-to-all(bf16[16,2,64,256]{3,2,1,0:T(8,128)(2,1)S(1)} %bitcast.3), channel_id=1, replica_groups=mesh['z'=8,'yl'=2,'c'=2,'yh'=2,'x'=4] {'yl','yh','x'}, dimensions={0} | all-to-all | bytes 2097152 | tf_op jit(solution)/shard_map/all_to_all | solution.py:314
  75.5 0.8 %convert_reduce_fusion = f32[2,64,256]{2,1,0:T(8,128)} fusion(bf16[16,2,64,256]{3,2,1,0:T(8,128)(2,1)S(1)} %all_to_all.5), kind=kLoop, calls=%fused_computation | loop fusion | flops 1015808 | bytes 1179648 | tf_op jit(solution)/shard_map/reduce_sum | solution.py:315
Async XLA Ops:
  0.0 14.4 %collective-permute-start.2 = (bf16[256,1024]{1,0:T(8,128)(2,1)}, bf16[256,1024]{1,0:T(8,128)(2,1)S(1)}, u32[]{:S(2)}, u32[]{:S(2)}) collective-permute-start(bf16[256,1024]{1,0:T(8,128)(2,1)} %refs_0_.1), channel_id=1, source_target_pairs={{0,0},{33,1},{66,2},{99,3},{132,4},{165,5},{198,6},{231,7},{8,8},{... | collective-permute-start | bytes 1572872 | tf_op jit(solution)/shard_map/ppermute | solution.py:44
  1.7 17.9 %collective-permute-start.4 = (bf16[256,1024]{1,0:T(8,128)(2,1)}, bf16[256,1024]{1,0:T(8,128)(2,1)S(1)}, u32[]{:S(2)}, u32[]{:S(2)}) collective-permute-start(bf16[256,1024]{1,0:T(8,128)(2,1)} %refs_7_.1), channel_id=1, source_target_pairs={{0,0},{33,1},{66,2},{99,3},{132,4},{165,5},{198,6},{231,7},{8,8},{... | collective-permute-start | bytes 1572872 | tf_op jit(solution)/shard_map/ppermute | solution.py:44
  3.4 21.6 %collective-permute-start.1 = (bf16[256,1024]{1,0:T(8,128)(2,1)}, bf16[256,1024]{1,0:T(8,128)(2,1)S(1)}, u32[]{:S(2)}, u32[]{:S(2)}) collective-permute-start(bf16[256,1024]{1,0:T(8,128)(2,1)} %refs_0_.1), channel_id=1, source_target_pairs={{16,0},{17,1},{18,2},{19,3},{20,4},{21,5},{22,6},{23,7},{24,8},{25... | collective-permute-start | bytes 1572872 | tf_op jit(solution)/shard_map/ppermute | solution.py:44
  14.4 11.3 %collective-permute-start.3 = (bf16[256,1024]{1,0:T(8,128)(2,1)S(1)}, bf16[256,1024]{1,0:T(8,128)(2,1)S(1)}, u32[]{:S(2)}, u32[]{:S(2)}) collective-permute-start(bf16[256,1024]{1,0:T(8,128)(2,1)S(1)} %collective-permute-done.2.s_own), channel_id=1, source_target_pairs={{8,0},{9,1},{10,2},{11,3},{12,4},{13,5},{14,6},{15,7},{0,8},{1,9},... | collective-permute-start | bytes 1572872 | tf_op jit(solution)/shard_map/ppermute | solution.py:44
  15.6 3.9 %collective-permute-start.6 = (bf16[256,512]{1,0:T(8,128)(2,1)}, bf16[256,512]{1,0:T(8,128)(2,1)S(1)}, u32[]{:S(2)}, u32[]{:S(2)}) collective-permute-start(bf16[256,512]{1,0:T(8,128)(2,1)} %param.11), channel_id=1, source_target_pairs={{0,0},{33,1},{66,2},{99,3},{132,4},{165,5},{198,6},{231,7},{8,8},{... | collective-permute-start | bytes 786440 | tf_op jit(solution)/shard_map/ppermute | solution.py:44
  17.2 28.9 %collective-permute-start = (bf16[256,1024]{1,0:T(8,128)(2,1)}, bf16[256,1024]{1,0:T(8,128)(2,1)S(1)}, u32[]{:S(2)}, u32[]{:S(2)}) collective-permute-start(bf16[256,1024]{1,0:T(8,128)(2,1)} %refs_7_.1), channel_id=1, source_target_pairs={{20,0},{21,1},{22,2},{23,3},{16,4},{17,5},{18,6},{19,7},{28,8},{29... | collective-permute-start | bytes 1572872 | tf_op jit(solution)/shard_map/ppermute | solution.py:44
  19.5 33.8 %collective-permute-start.7 = (bf16[256,512]{1,0:T(8,128)(2,1)S(1)}, bf16[256,512]{1,0:T(8,128)(2,1)S(1)}, u32[]{:S(2)}, u32[]{:S(2)}) collective-permute-start(bf16[256,512]{1,0:T(8,128)(2,1)S(1)} %collective-permute-done.6.s_ref), channel_id=1, source_target_pairs={{8,0},{9,1},{10,2},{11,3},{12,4},{13,5},{14,6},{15,7},{0,8},{1,9},... | collective-permute-start | bytes 786440 | tf_op jit(solution)/shard_map/ppermute | solution.py:44
  19.6 30.8 %collective-permute-start.5 = (bf16[256,1024]{1,0:T(8,128)(2,1)S(1)}, bf16[256,1024]{1,0:T(8,128)(2,1)S(1)}, u32[]{:S(2)}, u32[]{:S(2)}) collective-permute-start(bf16[256,1024]{1,0:T(8,128)(2,1)S(1)} %collective-permute-done.4.refs_4_), channel_id=1, source_target_pairs={{8,0},{9,1},{10,2},{11,3},{12,4},{13,5},{14,6},{15,7},{0,8},{1,9},... | collective-permute-start | bytes 1572872 | tf_op jit(solution)/shard_map/ppermute | solution.py:44

commit v4 on v3

--- a/solution.py
+++ b/solution.py
@@ -207,14 +207,14 @@
     )(own, near, s_own, s_other)
 
 
-def chi_kernel(part, cos_ref, kept_ref, own_ref, near_ref, s_ref, occ_ref, out_ref):
-    taus, points, _ = own_ref.shape
+def chi_kernel(part, rows_of, cos_ref, kept_ref, *refs):
+    sources, (s_ref, occ_ref, out_ref) = refs[:-3], refs[-3:]
+    taus, points, _ = sources[0].shape
     tiles = points // TILE
     here = slice(part * points, (part + 1) * points)
-    for i, source in enumerate((own_ref, near_ref)):
-
-        def body(t, i=i, source=source):
-            rows = pl.ds(i * points + t * TILE, TILE)
+    for place_at, (i, source) in enumerate(zip(rows_of, sources)):
+        for t in range(tiles):
+            rows = pl.ds(place_at * points + t * TILE, TILE)
             product = green(source, t, s_ref) * occ_ref[i * tiles + t, :, here]
             product = product.reshape(taus, TILE, points)
             for w in range(2):
@@ -226,51 +226,49 @@
                 out_ref[w, 0, rows, :] = high
                 out_ref[w, 1, rows, :] = (chi - high.astype(jnp.float32)).astype(jnp.bfloat16)
 
-        for t in range(tiles):
-            body(t)
-
-
-def chi_term(part, cos_rows, marks, own, near, s, green_occ):
-    taus, points, states = own.shape
+
+def chi_term(part, cos_rows, marks, blocks, s, green_occ):
+    taus, points, states = next(iter(blocks.values())).shape
 
     def kernel(*refs):
-        chi_kernel(part, *refs)
+        chi_kernel(part, tuple(blocks), *refs)
 
     return pl.pallas_call(
         kernel,
-        out_shape=jax.ShapeDtypeStruct((2, 2, 2 * points, points), jnp.bfloat16),
-        in_specs=[VMEM] * 6,
+        out_shape=jax.ShapeDtypeStruct((2, 2, len(blocks) * points, points), jnp.bfloat16),
+        in_specs=[VMEM] * (4 + len(blocks)),
         out_specs=VMEM,
         compiler_params=pltpu.CompilerParams(vmem_limit_bytes=24 * MIB),
-        cost_estimate=cost(4 * taus * points * points * states),
-    )(cos_rows, marks, own, near, s, green_occ)
-
-
-def answer_kernel(chi_ref, chi_other, s_ref, s_other, out_ref):
+        cost_estimate=cost(2 * len(blocks) * taus * points * points * states),
+    )(cos_rows, marks, *blocks.values(), s, green_occ)
+
+
+def answer_kernel(chi_ref, own_other, near_other, s_ref, s_other, out_ref):
     yl = lax.axis_index("yl")
     points = s_ref.shape[0]
     _, groups, _, width, _ = out_ref.shape
     for w in range(2):
         both = chi_ref[w].reshape(4 * points, points)
         answer = jnp.dot(both, s_ref[...], preferred_element_type=jnp.float32)
-        both = chi_other[w].reshape(4 * points, points)
-        answer = answer + jnp.dot(both, s_other[...], preferred_element_type=jnp.float32)
         answer = answer[: 2 * points] + answer[2 * points :]
-        for slot, part in ((yl, answer[:points]), (1 - yl, answer[points:])):
+        for i, (slot, other) in enumerate(((yl, own_other), (1 - yl, near_other))):
+            both = other[w].reshape(2 * points, points)
+            rest = jnp.dot(both, s_other[...], preferred_element_type=jnp.float32)
+            part = answer[i * points : (i + 1) * points] + rest[:points] + rest[points:]
             out_ref[slot, :, w] = part.T.astype(jnp.bfloat16).reshape(groups, width, points)
 
 
-def answer_term(chi, chi_other, s, s_other):
+def answer_term(chi, own_other, near_other, s, s_other):
     points, columns = s.shape
     groups = NYH * NX
     return pl.pallas_call(
         answer_kernel,
         out_shape=jax.ShapeDtypeStruct((NYL, groups, 2, columns // groups, points), jnp.bfloat16),
-        in_specs=[VMEM] * 4,
+        in_specs=[VMEM] * 5,
         out_specs=VMEM,
         compiler_params=pltpu.CompilerParams(vmem_limit_bytes=16 * MIB),
         cost_estimate=cost(32 * points * points * columns),
-    )(chi, chi_other, s, s_other)
+    )(chi, own_other, near_other, s, s_other)
 
 
 def per_device(
@@ -307,9 +305,10 @@
     green_occ = occ_term(occ_own, occ_next, occ_s, occ_t)
     vir_near, green_occ = lax.optimization_barrier((vir_near, green_occ))
     vir_own, vir_next = scaled(vir_decay, vir_held, vir_near)
-    chi_s = chi_term(0, cos_rows, marks, vir_own, vir_next, vir_s, green_occ)
-    chi_t = chi_term(1, cos_rows, marks, vir_own, vir_next, vir_t, green_occ)
-    parts = answer_term(chi_s, chi_t, col_s, col_t)
+    chi_s = chi_term(0, cos_rows, marks, {0: vir_own, 1: vir_next}, vir_s, green_occ)
+    chi_own = chi_term(1, cos_rows, marks, {0: vir_own}, vir_t, green_occ)
+    chi_near = chi_term(1, cos_rows, marks, {1: vir_next}, vir_t, green_occ)
+    parts = answer_term(chi_s, chi_own, chi_near, col_s, col_t)
     parts = parts.reshape(-1, *parts.shape[2:])
     spread = lax.all_to_all(parts, ("yl", "yh", "x"), split_axis=0, concat_axis=0, tiled=True)
     return spread.astype(jnp.float32).sum(axis=0)

time: 76.6 us -> 77 us (level)
    pallas_call x2 -> x3, Pallas kernels: 5.79 us -> 5.96 us  [chi_term(): pl.pallas_call(kernel, out_shape=jax.ShapeDtypeStruct((2, 2, len(blocks)...]
where the time goes in v4:
time: 77 us; the launch traced here: 76.7 us
  blocking collectives  21 us (27%)
  waiting for transfers between devices  20.7 us (27%)
  starting transfers between devices  18 us (23%)
  Pallas kernels  16.1 us (21%)
  other arithmetic  0.81 us (1%)
    all_to_all x1, blocking collectives, per_device(): lax.all_to_all(parts, ('yl', 'yh', 'x'), split_axis=0, concat_axis=0, til...  21 us
    ppermute x8, waiting for transfers between devices, take(): lax.ppermute(array, AXES, [(place(source(*at)), place(at)) for at in ever...  20.7 us
    ppermute x8, starting transfers between devices, take(): lax.ppermute(array, AXES, [(place(source(*at)), place(at)) for at in ever...  18 us
    pallas_call x3, Pallas kernels, chi_term(): pl.pallas_call(kernel, out_shape=jax.ShapeDtypeStruct((2, 2, len(blocks)...  5.96 us
    pallas_call x1, Pallas kernels, occ_term(): pl.pallas_call(occ_kernel, out_shape=jax.ShapeDtypeStruct((2 * points //...  4.53 us
    pallas_call x1, Pallas kernels, first_term(): pl.pallas_call(first_kernel, out_shape=(jax.ShapeDtypeStruct((taus, point...  2.26 us
    pallas_call x2, Pallas kernels, scaled(): pl.pallas_call(scale_kernel, out_shape=[jax.ShapeDtypeStruct((decay.shape...  2.03 us
  transfers between devices with their start and end apart: 8, of which 2 were waited for; matrix products, arithmetic and copies ran while one was open for 0% of the time, Pallas kernels for 19%

profile of v4, /device:TPU:1, one launch (start us, length us, event | category | flops | bytes accessed | tf_op | source)
XLA Modules:
  0.0 76.7 jit_solution(14174508685689260769)
XLA Ops:
  0.0 1.7 %collective-permute-start.2 = (bf16[256,1024]{1,0:T(8,128)(2,1)}, bf16[256,1024]{1,0:T(8,128)(2,1)S(1)}, u32[]{:S(2)}, u32[]{:S(2)}) collective-permute-start(bf16[256,1024]{1,0:T(8,128)(2,1)} %refs_0_.1), channel_id=1, source_target_pairs={{0,0},{33,1},{66,2},{99,3},{132,4},{165,5},{198,6},{231,7},{8,8},{... | collective-permute-start | bytes 1572872 | tf_op jit(solution)/shard_map/ppermute | solution.py:44
  1.7 1.7 %collective-permute-start.4 = (bf16[256,1024]{1,0:T(8,128)(2,1)}, bf16[256,1024]{1,0:T(8,128)(2,1)S(1)}, u32[]{:S(2)}, u32[]{:S(2)}) collective-permute-start(bf16[256,1024]{1,0:T(8,128)(2,1)} %refs_7_.1), channel_id=1, source_target_pairs={{0,0},{33,1},{66,2},{99,3},{132,4},{165,5},{198,6},{231,7},{8,8},{... | collective-permute-start | bytes 1572872 | tf_op jit(solution)/shard_map/ppermute | solution.py:44
  3.4 11.0 %collective-permute-start.1 = (bf16[256,1024]{1,0:T(8,128)(2,1)}, bf16[256,1024]{1,0:T(8,128)(2,1)S(1)}, u32[]{:S(2)}, u32[]{:S(2)}) collective-permute-start(bf16[256,1024]{1,0:T(8,128)(2,1)} %refs_0_.1), channel_id=1, source_target_pairs={{16,0},{17,1},{18,2},{19,3},{20,4},{21,5},{22,6},{23,7},{24,8},{25... | collective-permute-start | bytes 1572872 | tf_op jit(solution)/shard_map/ppermute | solution.py:44
  14.4 0.0 collective-permute-done.2.s_own
  14.4 1.2 %collective-permute-start.3 = (bf16[256,1024]{1,0:T(8,128)(2,1)S(1)}, bf16[256,1024]{1,0:T(8,128)(2,1)S(1)}, u32[]{:S(2)}, u32[]{:S(2)}) collective-permute-start(bf16[256,1024]{1,0:T(8,128)(2,1)S(1)} %collective-permute-done.2.s_own), channel_id=1, source_target_pairs={{8,0},{9,1},{10,2},{11,3},{12,4},{13,5},{14,6},{15,7},{0,8},{1,9},... | collective-permute-start | bytes 1572872 | tf_op jit(solution)/shard_map/ppermute | solution.py:44
  15.6 1.6 %collective-permute-start.6 = (bf16[256,512]{1,0:T(8,128)(2,1)}, bf16[256,512]{1,0:T(8,128)(2,1)S(1)}, u32[]{:S(2)}, u32[]{:S(2)}) collective-permute-start(bf16[256,512]{1,0:T(8,128)(2,1)} %param.11), channel_id=1, source_target_pairs={{0,0},{33,1},{66,2},{99,3},{132,4},{165,5},{198,6},{231,7},{8,8},{... | collective-permute-start | bytes 786440 | tf_op jit(solution)/shard_map/ppermute | solution.py:44
  17.2 0.0 collective-permute-start
  17.2 0.0 collective-permute-done.4.refs_4_
  17.2 0.0 collective-permute-start.5
  17.2 2.3 %shard_map.91 = (bf16[8,256,1024]{2,1,0:T(8,128)(2,1)S(1)}, f32[8,1024]{1,0:T(8,128)S(1)}, f32[8,1024]{1,0:T(8,128)S(1)}, f32[16,256]{1,0:T(8,128)S(1)}, f32[8,5...) custom-call(bf16[256,1024]{1,0:T(8,128)(2,1)} %refs_0_.1, f32[1,1024]{1,0:T(1,128)} %bitcast.4, f32[1,1024]{1,0:T(1,128)} %bitcast.5, ...), custom_call_target="tpu_custom_call" | custom-call | flops 100000000 | bytes 4194304 | tf_op jit(solution)/shard_map/pallas_call | solution.py:156
  19.5 0.0 collective-permute-done.6.s_ref
  19.5 0.8 collective-permute-start.7
  20.3 4.7 %collective-permute-done.1.refs_0_ = bf16[256,1024]{1,0:T(8,128)(2,1)S(1)} collective-permute-done((bf16[256,1024]{1,0:T(8,128)(2,1)}, bf16[256,1024]{1,0:T(8,128)(2,1)S(1)}, u32[]{:S(2)}, u32[]{:S(2)}) %collective-permute-start.1) | collective-permute-done | bytes 524320 | tf_op jit(solution)/shard_map/ppermute | solution.py:44
  25.0 0.7 shard_map.92.near_ref
  25.7 0.0 collective-permute-done.3.s_other
  25.7 4.5 %shard_map.93.refs_5_.refs_4_ = f32[4,1024,512]{2,1,0:T(8,128)S(1)} custom-call(bf16[8,256,1024]{2,1,0:T(8,128)(2,1)S(1)} %get-tuple-element.19.own_ref, bf16[8,256,1024]{2,1,0:T(8,128)(2,1)S(1)} %shard_map.92.near_ref, bf16[256,1024]{1,0:T(8,128)(2,1)S(1)} %collective-permute-done.2.s_own, bf16[256,1024]{1,0:T(8,128)(2,1)S(1)} %collective-permute-done.3.s_other), custom_call_target="tpu_custom_call" | custom-call | flops 4294967296 | bytes 4194304 | tf_op jit(solution)/shard_map/pallas_call | solution.py:200
  30.2 15.9 %collective-permute-done.refs_1_ = bf16[256,1024]{1,0:T(8,128)(2,1)S(1)} collective-permute-done((bf16[256,1024]{1,0:T(8,128)(2,1)}, bf16[256,1024]{1,0:T(8,128)(2,1)S(1)}, u32[]{:S(2)}, u32[]{:S(2)}) %collective-permute-start) | collective-permute-done | bytes 524320 | tf_op jit(solution)/shard_map/ppermute | solution.py:44
  46.1 1.4 %shard_map.94 = (bf16[8,256,1024]{2,1,0:T(8,128)(2,1)S(1)}, bf16[8,256,1024]{2,1,0:T(8,128)(2,1)S(1)}) custom-call(f32[8,1024]{1,0:T(8,128)S(1)} %get-tuple-element.17.decay_ref, bf16[256,1024]{1,0:T(8,128)(2,1)S(1)} %get-tuple-element.18.refs_0_, bf16[256,1024]{1,0:T(8,128)(2,1)S(1)} %collective-permute-done.refs_1_), custom_call_target="tpu_custom_call" | custom-call | flops 100000000 | bytes 4194304 | tf_op jit(solution)/shard_map/pallas_call | solution.py:86
  47.5 0.0 collective-permute-done.5.refs_3_
  47.5 1.5 %shard_map.96.own_other = bf16[2,2,256,256]{3,2,1,0:T(8,128)(2,1)S(1)} custom-call(f32[16,256]{1,0:T(8,128)S(1)} %get-tuple-element.15.refs_0_, f32[8,512]{1,0:T(8,128)S(1)} %get-tuple-element.16.refs_1_, bf16[8,256,1024]{2,1,0:T(8,128)(2,1)S(1)} %get-tuple-element.22.refs_2_, bf16[256,1024]{1,0:T(8,128)(2,1)S(1)} %collective-permute-done.5.refs_3_, ...), custom_call_target="tpu_custom_call" | custom-call | flops 1073741824 | bytes 4194304 | tf_op jit(solution)/shard_map/pallas_call | solution.py:236
  49.0 1.5 %shard_map.97.near_other = bf16[2,2,256,256]{3,2,1,0:T(8,128)(2,1)S(1)} custom-call(f32[16,256]{1,0:T(8,128)S(1)} %get-tuple-element.15.refs_0_, f32[8,512]{1,0:T(8,128)S(1)} %get-tuple-element.16.refs_1_, bf16[8,256,1024]{2,1,0:T(8,128)(2,1)S(1)} %get-tuple-element.23.refs_3_.refs_2_, bf16[256,1024]{1,0:T(8,128)(2,1)S(1)} %collective-permute-done.5.refs_3_, ...), custom_call_target="tpu_custom_call" | custom-call | flops 1073741824 | bytes 4194304 | tf_op jit(solution)/shard_map/pallas_call | solution.py:236
  50.6 2.9 %shard_map.95.chi_ref = bf16[2,2,512,256]{3,2,1,0:T(8,128)(2,1)S(1)} custom-call(f32[16,256]{1,0:T(8,128)S(1)} %get-tuple-element.15.refs_0_, f32[8,512]{1,0:T(8,128)S(1)} %get-tuple-element.16.refs_1_, bf16[8,256,1024]{2,1,0:T(8,128)(2,1)S(1)} %get-tuple-element.22.refs_2_, bf16[8,256,1024]{2,1,0:T(8,128)(2,1)S(1)} %get-tuple-element.23.refs_3_.refs_2_, ...), custom_call_target="tpu_custom_call" | custom-call | flops 2147483648 | bytes 4194304 | tf_op jit(solution)/shard_map/pallas_call | solution.py:236
  53.5 0.0 collective-permute-done.7.s_other
  53.5 1.3 %shard_map.98 = bf16[2,8,2,64,256]{4,3,2,1,0:T(8,128)(2,1)S(1)} custom-call(bf16[2,2,512,256]{3,2,1,0:T(8,128)(2,1)S(1)} %shard_map.95.chi_ref, bf16[2,2,256,256]{3,2,1,0:T(8,128)(2,1)S(1)} %shard_map.96.own_other, bf16[2,2,256,256]{3,2,1,0:T(8,128)(2,1)S(1)} %shard_map.97.near_other, bf16[256,512]{1,0:T(8,128)(2,1)S(1)} %collective-permute-done.6.s_ref, ...), custom_call_target="tpu_custom_call" | custom-call | flops 1073741824 | bytes 4194304 | tf_op jit(solution)/shard_map/pallas_call | solution.py:264
  54.8 21.0 %all_to_all.5 = bf16[16,2,64,256]{3,2,1,0:T(8,128)(2,1)S(1)} all-to-all(bf16[16,2,64,256]{3,2,1,0:T(8,128)(2,1)S(1)} %bitcast.3), channel_id=1, replica_groups=mesh['z'=8,'yl'=2,'c'=2,'yh'=2,'x'=4] {'yl','yh','x'}, dimensions={0} | all-to-all | bytes 2097152 | tf_op jit(solution)/shard_map/all_to_all | solution.py:313
  75.9 0.8 %convert_reduce_fusion = f32[2,64,256]{2,1,0:T(8,128)} fusion(bf16[16,2,64,256]{3,2,1,0:T(8,128)(2,1)S(1)} %all_to_all.5), kind=kLoop, calls=%fused_computation | loop fusion | flops 1015808 | bytes 1179648 | tf_op jit(solution)/shard_map/reduce_sum | solution.py:314
Async XLA Ops:
  0.0 14.4 %collective-permute-start.2 = (bf16[256,1024]{1,0:T(8,128)(2,1)}, bf16[256,1024]{1,0:T(8,128)(2,1)S(1)}, u32[]{:S(2)}, u32[]{:S(2)}) collective-permute-start(bf16[256,1024]{1,0:T(8,128)(2,1)} %refs_0_.1), channel_id=1, source_target_pairs={{0,0},{33,1},{66,2},{99,3},{132,4},{165,5},{198,6},{231,7},{8,8},{... | collective-permute-start | bytes 1572872 | tf_op jit(solution)/shard_map/ppermute | solution.py:44
  1.7 15.5 %collective-permute-start.4 = (bf16[256,1024]{1,0:T(8,128)(2,1)}, bf16[256,1024]{1,0:T(8,128)(2,1)S(1)}, u32[]{:S(2)}, u32[]{:S(2)}) collective-permute-start(bf16[256,1024]{1,0:T(8,128)(2,1)} %refs_7_.1), channel_id=1, source_target_pairs={{0,0},{33,1},{66,2},{99,3},{132,4},{165,5},{198,6},{231,7},{8,8},{... | collective-permute-start | bytes 1572872 | tf_op jit(solution)/shard_map/ppermute | solution.py:44
  3.4 21.6 %collective-permute-start.1 = (bf16[256,1024]{1,0:T(8,128)(2,1)}, bf16[256,1024]{1,0:T(8,128)(2,1)S(1)}, u32[]{:S(2)}, u32[]{:S(2)}) collective-permute-start(bf16[256,1024]{1,0:T(8,128)(2,1)} %refs_0_.1), channel_id=1, source_target_pairs={{16,0},{17,1},{18,2},{19,3},{20,4},{21,5},{22,6},{23,7},{24,8},{25... | collective-permute-start | bytes 1572872 | tf_op jit(solution)/shard_map/ppermute | solution.py:44
  14.4 11.3 %collective-permute-start.3 = (bf16[256,1024]{1,0:T(8,128)(2,1)S(1)}, bf16[256,1024]{1,0:T(8,128)(2,1)S(1)}, u32[]{:S(2)}, u32[]{:S(2)}) collective-permute-start(bf16[256,1024]{1,0:T(8,128)(2,1)S(1)} %collective-permute-done.2.s_own), channel_id=1, source_target_pairs={{8,0},{9,1},{10,2},{11,3},{12,4},{13,5},{14,6},{15,7},{0,8},{1,9},... | collective-permute-start | bytes 1572872 | tf_op jit(solution)/shard_map/ppermute | solution.py:44
  15.6 3.9 %collective-permute-start.6 = (bf16[256,512]{1,0:T(8,128)(2,1)}, bf16[256,512]{1,0:T(8,128)(2,1)S(1)}, u32[]{:S(2)}, u32[]{:S(2)}) collective-permute-start(bf16[256,512]{1,0:T(8,128)(2,1)} %param.11), channel_id=1, source_target_pairs={{0,0},{33,1},{66,2},{99,3},{132,4},{165,5},{198,6},{231,7},{8,8},{... | collective-permute-start | bytes 786440 | tf_op jit(solution)/shard_map/ppermute | solution.py:44
  17.2 28.9 %collective-permute-start = (bf16[256,1024]{1,0:T(8,128)(2,1)}, bf16[256,1024]{1,0:T(8,128)(2,1)S(1)}, u32[]{:S(2)}, u32[]{:S(2)}) collective-permute-start(bf16[256,1024]{1,0:T(8,128)(2,1)} %refs_7_.1), channel_id=1, source_target_pairs={{20,0},{21,1},{22,2},{23,3},{16,4},{17,5},{18,6},{19,7},{28,8},{29... | collective-permute-start | bytes 1572872 | tf_op jit(solution)/shard_map/ppermute | solution.py:44
  17.2 30.3 %collective-permute-start.5 = (bf16[256,1024]{1,0:T(8,128)(2,1)S(1)}, bf16[256,1024]{1,0:T(8,128)(2,1)S(1)}, u32[]{:S(2)}, u32[]{:S(2)}) collective-permute-start(bf16[256,1024]{1,0:T(8,128)(2,1)S(1)} %collective-permute-done.4.refs_4_), channel_id=1, source_target_pairs={{8,0},{9,1},{10,2},{11,3},{12,4},{13,5},{14,6},{15,7},{0,8},{1,9},... | collective-permute-start | bytes 1572872 | tf_op jit(solution)/shard_map/ppermute | solution.py:44
  19.5 34.0 %collective-permute-start.7 = (bf16[256,512]{1,0:T(8,128)(2,1)S(1)}, bf16[256,512]{1,0:T(8,128)(2,1)S(1)}, u32[]{:S(2)}, u32[]{:S(2)}) collective-permute-start(bf16[256,512]{1,0:T(8,128)(2,1)S(1)} %collective-permute-done.6.s_ref), channel_id=1, source_target_pairs={{8,0},{9,1},{10,2},{11,3},{12,4},{13,5},{14,6},{15,7},{0,8},{1,9},... | collective-permute-start | bytes 786440 | tf_op jit(solution)/shard_map/ppermute | solution.py:44

commit v5 on v4

--- a/solution.py
+++ b/solution.py
@@ -246,7 +246,7 @@
 def answer_kernel(chi_ref, own_other, near_other, s_ref, s_other, out_ref):
     yl = lax.axis_index("yl")
     points = s_ref.shape[0]
-    _, groups, _, width, _ = out_ref.shape
+    groups, _, _, width, _ = out_ref.shape
     for w in range(2):
         both = chi_ref[w].reshape(4 * points, points)
         answer = jnp.dot(both, s_ref[...], preferred_element_type=jnp.float32)
@@ -255,7 +255,7 @@
             both = other[w].reshape(2 * points, points)
             rest = jnp.dot(both, s_other[...], preferred_element_type=jnp.float32)
             part = answer[i * points : (i + 1) * points] + rest[:points] + rest[points:]
-            out_ref[slot, :, w] = part.T.astype(jnp.bfloat16).reshape(groups, width, points)
+            out_ref[:, slot, w] = part.T.astype(jnp.bfloat16).reshape(groups, width, points)
 
 
 def answer_term(chi, own_other, near_other, s, s_other):
@@ -263,7 +263,7 @@
     groups = NYH * NX
     return pl.pallas_call(
         answer_kernel,
-        out_shape=jax.ShapeDtypeStruct((NYL, groups, 2, columns // groups, points), jnp.bfloat16),
+        out_shape=jax.ShapeDtypeStruct((groups, NYL, 2, columns // groups, points), jnp.bfloat16),
         in_specs=[VMEM] * 5,
         out_specs=VMEM,
         compiler_params=pltpu.CompilerParams(vmem_limit_bytes=16 * MIB),
@@ -310,7 +310,7 @@
     chi_near = chi_term(1, cos_rows, marks, {1: vir_next}, vir_t, green_occ)
     parts = answer_term(chi_s, chi_own, chi_near, col_s, col_t)
     parts = parts.reshape(-1, *parts.shape[2:])
-    spread = lax.all_to_all(parts, ("yl", "yh", "x"), split_axis=0, concat_axis=0, tiled=True)
+    spread = lax.all_to_all(parts, ("yh", "x", "yl"), split_axis=0, concat_axis=0, tiled=True)
     return spread.astype(jnp.float32).sum(axis=0)
 
 

time: 77 us -> 77 us (level)
  no operation moved by 1% of the time
where the time goes in v5:
time: 77 us; the launch traced here: 76.7 us
  blocking collectives  21.1 us (27%)
  waiting for transfers between devices  20.7 us (27%)
  starting transfers between devices  18 us (23%)
  Pallas kernels  16.1 us (21%)
  other arithmetic  0.81 us (1%)
    all_to_all x1, blocking collectives, per_device(): lax.all_to_all(parts, ('yh', 'x', 'yl'), split_axis=0, concat_axis=0, til...  21.1 us
    ppermute x8, waiting for transfers between devices, take(): lax.ppermute(array, AXES, [(place(source(*at)), place(at)) for at in ever...  20.7 us
    ppermute x8, starting transfers between devices, take(): lax.ppermute(array, AXES, [(place(source(*at)), place(at)) for at in ever...  18 us
    pallas_call x3, Pallas kernels, chi_term(): pl.pallas_call(kernel, out_shape=jax.ShapeDtypeStruct((2, 2, len(blocks)...  5.96 us
    pallas_call x1, Pallas kernels, occ_term(): pl.pallas_call(occ_kernel, out_shape=jax.ShapeDtypeStruct((2 * points //...  4.53 us
    pallas_call x1, Pallas kernels, first_term(): pl.pallas_call(first_kernel, out_shape=(jax.ShapeDtypeStruct((taus, point...  2.26 us
    pallas_call x2, Pallas kernels, scaled(): pl.pallas_call(scale_kernel, out_shape=[jax.ShapeDtypeStruct((decay.shape...  2.03 us
  transfers between devices with their start and end apart: 8, of which 2 were waited for; matrix products, arithmetic and copies ran while one was open for 0% of the time, Pallas kernels for 19%

profile of v5, /device:TPU:1, one launch (start us, length us, event | category | flops | bytes accessed | tf_op | source)
XLA Modules:
  0.0 76.7 jit_solution(7575572610622014082)
XLA Ops:
  0.0 1.7 %collective-permute-start.2 = (bf16[256,1024]{1,0:T(8,128)(2,1)}, bf16[256,1024]{1,0:T(8,128)(2,1)S(1)}, u32[]{:S(2)}, u32[]{:S(2)}) collective-permute-start(bf16[256,1024]{1,0:T(8,128)(2,1)} %refs_0_.1), channel_id=1, source_target_pairs={{0,0},{33,1},{66,2},{99,3},{132,4},{165,5},{198,6},{231,7},{8,8},{... | collective-permute-start | bytes 1572872 | tf_op jit(solution)/shard_map/ppermute | solution.py:44
  1.7 1.7 %collective-permute-start.4 = (bf16[256,1024]{1,0:T(8,128)(2,1)}, bf16[256,1024]{1,0:T(8,128)(2,1)S(1)}, u32[]{:S(2)}, u32[]{:S(2)}) collective-permute-start(bf16[256,1024]{1,0:T(8,128)(2,1)} %refs_7_.1), channel_id=1, source_target_pairs={{0,0},{33,1},{66,2},{99,3},{132,4},{165,5},{198,6},{231,7},{8,8},{... | collective-permute-start | bytes 1572872 | tf_op jit(solution)/shard_map/ppermute | solution.py:44
  3.4 11.0 %collective-permute-start.1 = (bf16[256,1024]{1,0:T(8,128)(2,1)}, bf16[256,1024]{1,0:T(8,128)(2,1)S(1)}, u32[]{:S(2)}, u32[]{:S(2)}) collective-permute-start(bf16[256,1024]{1,0:T(8,128)(2,1)} %refs_0_.1), channel_id=1, source_target_pairs={{16,0},{17,1},{18,2},{19,3},{20,4},{21,5},{22,6},{23,7},{24,8},{25... | collective-permute-start | bytes 1572872 | tf_op jit(solution)/shard_map/ppermute | solution.py:44
  14.4 0.0 collective-permute-done.2.s_own
  14.4 1.2 %collective-permute-start.3 = (bf16[256,1024]{1,0:T(8,128)(2,1)S(1)}, bf16[256,1024]{1,0:T(8,128)(2,1)S(1)}, u32[]{:S(2)}, u32[]{:S(2)}) collective-permute-start(bf16[256,1024]{1,0:T(8,128)(2,1)S(1)} %collective-permute-done.2.s_own), channel_id=1, source_target_pairs={{8,0},{9,1},{10,2},{11,3},{12,4},{13,5},{14,6},{15,7},{0,8},{1,9},... | collective-permute-start | bytes 1572872 | tf_op jit(solution)/shard_map/ppermute | solution.py:44
  15.6 1.6 %collective-permute-start.6 = (bf16[256,512]{1,0:T(8,128)(2,1)}, bf16[256,512]{1,0:T(8,128)(2,1)S(1)}, u32[]{:S(2)}, u32[]{:S(2)}) collective-permute-start(bf16[256,512]{1,0:T(8,128)(2,1)} %param.11), channel_id=1, source_target_pairs={{0,0},{33,1},{66,2},{99,3},{132,4},{165,5},{198,6},{231,7},{8,8},{... | collective-permute-start | bytes 786440 | tf_op jit(solution)/shard_map/ppermute | solution.py:44
  17.2 0.0 collective-permute-start
  17.2 0.0 collective-permute-done.4.refs_4_
  17.2 0.0 collective-permute-start.5
  17.2 2.3 %shard_map.91 = (bf16[8,256,1024]{2,1,0:T(8,128)(2,1)S(1)}, f32[8,1024]{1,0:T(8,128)S(1)}, f32[8,1024]{1,0:T(8,128)S(1)}, f32[16,256]{1,0:T(8,128)S(1)}, f32[8,5...) custom-call(bf16[256,1024]{1,0:T(8,128)(2,1)} %refs_0_.1, f32[1,1024]{1,0:T(1,128)} %bitcast.4, f32[1,1024]{1,0:T(1,128)} %bitcast.5, ...), custom_call_target="tpu_custom_call" | custom-call | flops 100000000 | bytes 4194304 | tf_op jit(solution)/shard_map/pallas_call | solution.py:156
  19.5 0.0 collective-permute-done.6.s_ref
  19.5 0.8 collective-permute-start.7
  20.3 4.7 %collective-permute-done.1.refs_0_ = bf16[256,1024]{1,0:T(8,128)(2,1)S(1)} collective-permute-done((bf16[256,1024]{1,0:T(8,128)(2,1)}, bf16[256,1024]{1,0:T(8,128)(2,1)S(1)}, u32[]{:S(2)}, u32[]{:S(2)}) %collective-permute-start.1) | collective-permute-done | bytes 524320 | tf_op jit(solution)/shard_map/ppermute | solution.py:44
  25.0 0.7 shard_map.92.near_ref
  25.7 0.0 collective-permute-done.3.s_other
  25.7 4.5 %shard_map.93.refs_5_.refs_4_ = f32[4,1024,512]{2,1,0:T(8,128)S(1)} custom-call(bf16[8,256,1024]{2,1,0:T(8,128)(2,1)S(1)} %get-tuple-element.19.own_ref, bf16[8,256,1024]{2,1,0:T(8,128)(2,1)S(1)} %shard_map.92.near_ref, bf16[256,1024]{1,0:T(8,128)(2,1)S(1)} %collective-permute-done.2.s_own, bf16[256,1024]{1,0:T(8,128)(2,1)S(1)} %collective-permute-done.3.s_other), custom_call_target="tpu_custom_call" | custom-call | flops 4294967296 | bytes 4194304 | tf_op jit(solution)/shard_map/pallas_call | solution.py:200
  30.2 15.9 %collective-permute-done.refs_1_ = bf16[256,1024]{1,0:T(8,128)(2,1)S(1)} collective-permute-done((bf16[256,1024]{1,0:T(8,128)(2,1)}, bf16[256,1024]{1,0:T(8,128)(2,1)S(1)}, u32[]{:S(2)}, u32[]{:S(2)}) %collective-permute-start) | collective-permute-done | bytes 524320 | tf_op jit(solution)/shard_map/ppermute | solution.py:44
  46.1 1.4 %shard_map.94 = (bf16[8,256,1024]{2,1,0:T(8,128)(2,1)S(1)}, bf16[8,256,1024]{2,1,0:T(8,128)(2,1)S(1)}) custom-call(f32[8,1024]{1,0:T(8,128)S(1)} %get-tuple-element.17.decay_ref, bf16[256,1024]{1,0:T(8,128)(2,1)S(1)} %get-tuple-element.18.refs_0_, bf16[256,1024]{1,0:T(8,128)(2,1)S(1)} %collective-permute-done.refs_1_), custom_call_target="tpu_custom_call" | custom-call | flops 100000000 | bytes 4194304 | tf_op jit(solution)/shard_map/pallas_call | solution.py:86
  47.5 0.0 collective-permute-done.5.refs_3_
  47.5 1.5 %shard_map.96.own_other = bf16[2,2,256,256]{3,2,1,0:T(8,128)(2,1)S(1)} custom-call(f32[16,256]{1,0:T(8,128)S(1)} %get-tuple-element.15.refs_0_, f32[8,512]{1,0:T(8,128)S(1)} %get-tuple-element.16.refs_1_, bf16[8,256,1024]{2,1,0:T(8,128)(2,1)S(1)} %get-tuple-element.22.refs_2_, bf16[256,1024]{1,0:T(8,128)(2,1)S(1)} %collective-permute-done.5.refs_3_, ...), custom_call_target="tpu_custom_call" | custom-call | flops 1073741824 | bytes 4194304 | tf_op jit(solution)/shard_map/pallas_call | solution.py:236
  49.0 1.5 %shard_map.97.near_other = bf16[2,2,256,256]{3,2,1,0:T(8,128)(2,1)S(1)} custom-call(f32[16,256]{1,0:T(8,128)S(1)} %get-tuple-element.15.refs_0_, f32[8,512]{1,0:T(8,128)S(1)} %get-tuple-element.16.refs_1_, bf16[8,256,1024]{2,1,0:T(8,128)(2,1)S(1)} %get-tuple-element.23.refs_3_.refs_2_, bf16[256,1024]{1,0:T(8,128)(2,1)S(1)} %collective-permute-done.5.refs_3_, ...), custom_call_target="tpu_custom_call" | custom-call | flops 1073741824 | bytes 4194304 | tf_op jit(solution)/shard_map/pallas_call | solution.py:236
  50.6 2.9 %shard_map.95.chi_ref = bf16[2,2,512,256]{3,2,1,0:T(8,128)(2,1)S(1)} custom-call(f32[16,256]{1,0:T(8,128)S(1)} %get-tuple-element.15.refs_0_, f32[8,512]{1,0:T(8,128)S(1)} %get-tuple-element.16.refs_1_, bf16[8,256,1024]{2,1,0:T(8,128)(2,1)S(1)} %get-tuple-element.22.refs_2_, bf16[8,256,1024]{2,1,0:T(8,128)(2,1)S(1)} %get-tuple-element.23.refs_3_.refs_2_, ...), custom_call_target="tpu_custom_call" | custom-call | flops 2147483648 | bytes 4194304 | tf_op jit(solution)/shard_map/pallas_call | solution.py:236
  53.5 0.0 collective-permute-done.7.s_other
  53.5 1.3 %shard_map.98 = bf16[8,2,2,64,256]{4,3,2,1,0:T(8,128)(2,1)S(1)} custom-call(bf16[2,2,512,256]{3,2,1,0:T(8,128)(2,1)S(1)} %shard_map.95.chi_ref, bf16[2,2,256,256]{3,2,1,0:T(8,128)(2,1)S(1)} %shard_map.96.own_other, bf16[2,2,256,256]{3,2,1,0:T(8,128)(2,1)S(1)} %shard_map.97.near_other, bf16[256,512]{1,0:T(8,128)(2,1)S(1)} %collective-permute-done.6.s_ref, ...), custom_call_target="tpu_custom_call" | custom-call | flops 1073741824 | bytes 4194304 | tf_op jit(solution)/shard_map/pallas_call | solution.py:264
  54.8 21.1 %all_to_all.5 = bf16[16,2,64,256]{3,2,1,0:T(8,128)(2,1)S(1)} all-to-all(bf16[16,2,64,256]{3,2,1,0:T(8,128)(2,1)S(1)} %bitcast.3), channel_id=1, replica_groups=mesh['z'=8,'yl'=2,'c'=2,'yh'=2,'x'=4] {'yh','x','yl'}, dimensions={0} | all-to-all | bytes 2097152 | tf_op jit(solution)/shard_map/all_to_all | solution.py:313
  75.9 0.8 %convert_reduce_fusion = f32[2,64,256]{2,1,0:T(8,128)} fusion(bf16[16,2,64,256]{3,2,1,0:T(8,128)(2,1)S(1)} %all_to_all.5), kind=kLoop, calls=%fused_computation | loop fusion | flops 1015808 | bytes 1179648 | tf_op jit(solution)/shard_map/reduce_sum | solution.py:314
Async XLA Ops:
  0.0 14.4 %collective-permute-start.2 = (bf16[256,1024]{1,0:T(8,128)(2,1)}, bf16[256,1024]{1,0:T(8,128)(2,1)S(1)}, u32[]{:S(2)}, u32[]{:S(2)}) collective-permute-start(bf16[256,1024]{1,0:T(8,128)(2,1)} %refs_0_.1), channel_id=1, source_target_pairs={{0,0},{33,1},{66,2},{99,3},{132,4},{165,5},{198,6},{231,7},{8,8},{... | collective-permute-start | bytes 1572872 | tf_op jit(solution)/shard_map/ppermute | solution.py:44
  1.7 15.5 %collective-permute-start.4 = (bf16[256,1024]{1,0:T(8,128)(2,1)}, bf16[256,1024]{1,0:T(8,128)(2,1)S(1)}, u32[]{:S(2)}, u32[]{:S(2)}) collective-permute-start(bf16[256,1024]{1,0:T(8,128)(2,1)} %refs_7_.1), channel_id=1, source_target_pairs={{0,0},{33,1},{66,2},{99,3},{132,4},{165,5},{198,6},{231,7},{8,8},{... | collective-permute-start | bytes 1572872 | tf_op jit(solution)/shard_map/ppermute | solution.py:44
  3.4 21.6 %collective-permute-start.1 = (bf16[256,1024]{1,0:T(8,128)(2,1)}, bf16[256,1024]{1,0:T(8,128)(2,1)S(1)}, u32[]{:S(2)}, u32[]{:S(2)}) collective-permute-start(bf16[256,1024]{1,0:T(8,128)(2,1)} %refs_0_.1), channel_id=1, source_target_pairs={{16,0},{17,1},{18,2},{19,3},{20,4},{21,5},{22,6},{23,7},{24,8},{25... | collective-permute-start | bytes 1572872 | tf_op jit(solution)/shard_map/ppermute | solution.py:44
  14.4 11.3 %collective-permute-start.3 = (bf16[256,1024]{1,0:T(8,128)(2,1)S(1)}, bf16[256,1024]{1,0:T(8,128)(2,1)S(1)}, u32[]{:S(2)}, u32[]{:S(2)}) collective-permute-start(bf16[256,1024]{1,0:T(8,128)(2,1)S(1)} %collective-permute-done.2.s_own), channel_id=1, source_target_pairs={{8,0},{9,1},{10,2},{11,3},{12,4},{13,5},{14,6},{15,7},{0,8},{1,9},... | collective-permute-start | bytes 1572872 | tf_op jit(solution)/shard_map/ppermute | solution.py:44
  15.6 3.9 %collective-permute-start.6 = (bf16[256,512]{1,0:T(8,128)(2,1)}, bf16[256,512]{1,0:T(8,128)(2,1)S(1)}, u32[]{:S(2)}, u32[]{:S(2)}) collective-permute-start(bf16[256,512]{1,0:T(8,128)(2,1)} %param.11), channel_id=1, source_target_pairs={{0,0},{33,1},{66,2},{99,3},{132,4},{165,5},{198,6},{231,7},{8,8},{... | collective-permute-start | bytes 786440 | tf_op jit(solution)/shard_map/ppermute | solution.py:44
  17.2 28.9 %collective-permute-start = (bf16[256,1024]{1,0:T(8,128)(2,1)}, bf16[256,1024]{1,0:T(8,128)(2,1)S(1)}, u32[]{:S(2)}, u32[]{:S(2)}) collective-permute-start(bf16[256,1024]{1,0:T(8,128)(2,1)} %refs_7_.1), channel_id=1, source_target_pairs={{20,0},{21,1},{22,2},{23,3},{16,4},{17,5},{18,6},{19,7},{28,8},{29... | collective-permute-start | bytes 1572872 | tf_op jit(solution)/shard_map/ppermute | solution.py:44
  17.2 30.3 %collective-permute-start.5 = (bf16[256,1024]{1,0:T(8,128)(2,1)S(1)}, bf16[256,1024]{1,0:T(8,128)(2,1)S(1)}, u32[]{:S(2)}, u32[]{:S(2)}) collective-permute-start(bf16[256,1024]{1,0:T(8,128)(2,1)S(1)} %collective-permute-done.4.refs_4_), channel_id=1, source_target_pairs={{8,0},{9,1},{10,2},{11,3},{12,4},{13,5},{14,6},{15,7},{0,8},{1,9},... | collective-permute-start | bytes 1572872 | tf_op jit(solution)/shard_map/ppermute | solution.py:44
  19.5 34.0 %collective-permute-start.7 = (bf16[256,512]{1,0:T(8,128)(2,1)S(1)}, bf16[256,512]{1,0:T(8,128)(2,1)S(1)}, u32[]{:S(2)}, u32[]{:S(2)}) collective-permute-start(bf16[256,512]{1,0:T(8,128)(2,1)S(1)} %collective-permute-done.6.s_ref), channel_id=1, source_target_pairs={{8,0},{9,1},{10,2},{11,3},{12,4},{13,5},{14,6},{15,7},{0,8},{1,9},... | collective-permute-start | bytes 786440 | tf_op jit(solution)/shard_map/ppermute | solution.py:44
